TPU v7x, 16 devices: a whole 2x2x2 slice. The times are simulated.
16 devices in a mesh: rep: 2 (over z), dp: 8 (over y, x, core).
Axes of the slice: x: 2, y: 2, z: 2, core: 2. Of those that a mesh axis runs over, the one named last changes fastest.
Arguments:
- hidden: bfloat16 [1024, 7168], P(('rep', 'dp')), parts along dimension 0
- ckv_cache: bfloat16 [1024, 256, 512], P(('rep', 'dp')), parts along dimension 0
- kpe_cache: bfloat16 [1024, 256, 64], P(('rep', 'dp')), parts along dimension 0
- cache_len: int32 [1024], P(('rep', 'dp')), parts along dimension 0
- rope_cos: float32 [1024, 32], P(('rep', 'dp')), parts along dimension 0
- rope_sin: float32 [1024, 32], P(('rep', 'dp')), parts along dimension 0
- norm_attn: float32 [7168], replicated
- w_dq: bfloat16 [7168, 1536], replicated
- norm_q: float32 [1536], replicated
- w_uq: bfloat16 [1536, 128, 192], replicated
- w_dkv: bfloat16 [7168, 576], replicated
- norm_kv: float32 [512], replicated
- w_uk: bfloat16 [512, 128, 128], replicated
- w_uv: bfloat16 [512, 128, 128], replicated
- w_out: bfloat16 [128, 128, 7168], replicated
- norm_mlp: float32 [7168], replicated
- w_gate: bfloat16 [7168, 18432], P(None, 'dp')
- w_up: bfloat16 [7168, 18432], P(None, 'dp')
- w_down: bfloat16 [18432, 7168], P('dp')
Outputs:
- output 1: bfloat16 [1024, 7168], P(('rep', 'dp')), parts along dimension 0
- output 2: bfloat16 [1024, 512], P(('rep', 'dp')), parts along dimension 0
- output 3: bfloat16 [1024, 64], P(('rep', 'dp')), parts along dimension 0
There are 2 independent parts. A program takes and returns all parts, laid end to end along the dimension named above; an argument that names none is the same for every part.
All inputs are finite; a program needn't handle non-finite values.
Results may differ from a plain program's by a relative error of at most 0.0109083.
Values are sent between devices in bfloat16 or wider.
A program may use at most 2 GiB of HBM per device.

v0:
```python
import math
import jax
import jax.numpy as jnp
from jax import lax
from jax.sharding import PartitionSpec as P

EPSILON = 1e-6
MSCALE = 0.1 * math.log(40.0) + 1.0


def rms_norm(values_in, gain_vec):
    floats = values_in.astype(jnp.float32)
    mean_sq = jnp.mean(floats * floats, axis=-1, keepdims=True)
    return floats * lax.rsqrt(mean_sq + EPSILON) * gain_vec


def apply_rope(values_in, cos_t, sin_t):
    half_dim = values_in.shape[-1] // 2
    low_half = values_in[..., :half_dim]
    high_half = values_in[..., half_dim:]
    return jnp.concatenate([low_half * cos_t - high_half * sin_t, high_half * cos_t + low_half * sin_t], axis=-1)


def attention_rows(hidden, ckv_cache, kpe_cache, cache_len, rope_cos, rope_sin, norm_attn, w_dq, norm_q, w_uq, w_dkv, norm_kv, w_uk, w_uv, w_out):
    nope_dim = w_uk.shape[2]
    value_a7 = w_uk.shape[0]
    score_scale = MSCALE * MSCALE / math.sqrt(w_uq.shape[2])
    normed = rms_norm(hidden, norm_attn).astype(jnp.bfloat16)
    q_latent = rms_norm(jnp.dot(normed, w_dq, preferred_element_type=jnp.float32), norm_q).astype(jnp.bfloat16)
    q_full = jnp.einsum('bl,lhe->bhe', q_latent, w_uq, preferred_element_type=jnp.float32)
    q_nope = q_full[..., :nope_dim].astype(jnp.bfloat16)
    q_pe = apply_rope(q_full[..., nope_dim:], rope_cos[:, None, :], rope_sin[:, None, :]).astype(jnp.bfloat16)
    kv_full = jnp.dot(normed, w_dkv, preferred_element_type=jnp.float32)
    ckv_new = rms_norm(kv_full[:, :value_a7], norm_kv).astype(jnp.bfloat16)
    kpe_new = apply_rope(kv_full[:, value_a7:], rope_cos, rope_sin).astype(jnp.bfloat16)
    q_abs = jnp.einsum('bhn,lhn->bhl', q_nope, w_uk, preferred_element_type=jnp.float32).astype(jnp.bfloat16)
    scores = (jnp.einsum('bhl,btl->bht', q_abs, ckv_cache, preferred_element_type=jnp.float32)
              + jnp.einsum('bhr,btr->bht', q_pe, kpe_cache, preferred_element_type=jnp.float32)) * score_scale
    positions = jnp.arange(ckv_cache.shape[1])
    scores = jnp.where(positions[None, None, :] < cache_len[:, None, None], scores, -jnp.inf)
    score_new = (jnp.einsum('bhl,bl->bh', q_abs, ckv_new, preferred_element_type=jnp.float32)
                 + jnp.einsum('bhr,br->bh', q_pe, kpe_new, preferred_element_type=jnp.float32)) * score_scale
    row_max = jnp.maximum(jnp.max(scores, axis=-1), score_new)
    exp_cache = jnp.exp(scores - row_max[..., None])
    exp_new = jnp.exp(score_new - row_max)
    norm_sum = jnp.sum(exp_cache, axis=-1) + exp_new
    weighted = (jnp.einsum('bht,btl->bhl', exp_cache.astype(jnp.bfloat16), ckv_cache, preferred_element_type=jnp.float32)
                + exp_new.astype(jnp.bfloat16).astype(jnp.float32)[..., None] * ckv_new.astype(jnp.float32)[:, None, :])
    lat_out = (weighted / norm_sum[..., None]).astype(jnp.bfloat16)
    head_out = jnp.einsum('bhl,lhv->bhv', lat_out, w_uv, preferred_element_type=jnp.float32).astype(jnp.bfloat16)
    attn_out = jnp.einsum('bhv,hvd->bd', head_out, w_out, preferred_element_type=jnp.float32)
    residual = (hidden.astype(jnp.float32) + attn_out).astype(jnp.bfloat16)
    return residual, ckv_new, kpe_new


def solution(mesh):
    row_spec = P(('rep', 'dp'), None)
    cube_spec = P(('rep', 'dp'), None, None)
    full_spec = P()
    in_specs = (row_spec, cube_spec, cube_spec, P(('rep', 'dp')), row_spec, row_spec,
                full_spec, full_spec, full_spec, full_spec, full_spec, full_spec, full_spec, full_spec, full_spec, full_spec,
                P(None, 'dp'), P(None, 'dp'), P('dp', None))

    def local_step(hidden, ckv_cache, kpe_cache, cache_len, rope_cos, rope_sin, norm_attn, w_dq, norm_q, w_uq, w_dkv, norm_kv, w_uk, w_uv, w_out, norm_mlp, w_gate, w_up, w_down):
        residual, ckv_new, kpe_new = attention_rows(hidden, ckv_cache, kpe_cache, cache_len, rope_cos, rope_sin, norm_attn, w_dq, norm_q, w_uq, w_dkv, norm_kv, w_uk, w_uv, w_out)
        mlp_in = rms_norm(residual, norm_mlp).astype(jnp.bfloat16)
        group_in = lax.all_gather(mlp_in, 'dp', axis=0, tiled=True)
        gate_val = jnp.dot(group_in, w_gate, preferred_element_type=jnp.float32)
        up_val = jnp.dot(group_in, w_up, preferred_element_type=jnp.float32)
        act_val = (jax.nn.silu(gate_val) * up_val).astype(jnp.bfloat16)
        partial_sum = jnp.dot(act_val, w_down, preferred_element_type=jnp.float32)
        mlp_rows = lax.psum_scatter(partial_sum, 'dp', scatter_dimension=0, tiled=True)
        out_hidden = (residual.astype(jnp.float32) + mlp_rows).astype(jnp.bfloat16)
        return out_hidden, ckv_new, kpe_new

    return jax.shard_map(local_step, mesh=mesh, in_specs=in_specs, out_specs=(row_spec, row_spec, row_spec), check_vma=False)
```

profile of v0, /device:TPU:0, one launch (start us, length us, event | category | flops | bytes accessed | tf_op | source)
XLA Modules:
  0.0 558.9 jit_solution(14240995404505898841)
XLA Ops:
  7.2 0.0 copy-start
  7.2 0.0 copy-start.3
  7.2 0.0 copy-start.7
  7.2 0.0 copy-start.13
  7.2 0.0 all-gather.2.cloned.1.call-start
  7.3 1.6 fusion.34
  8.9 6.2 %fusion.41 = f32[64,576]{1,0:T(8,128)S(1)} fusion(bf16[7168,576]{0,1:T(8,128)(2,1)} %param.29, bf16[64,7168]{1,0:T(8,128)(2,1)} %param.19, f32[7168]{0:T(1024)} %param.25, f32[64]{0:T(128)S(1)} %add_rsqrt_fusion.3), kind=kOutput, calls=%fused_computation.47 | convolution fusion | flops 530317312 | bytes 9351424 | tf_op jit(solution)/shard_map/dot_general | solution.py:33
  15.1 0.0 copy-start.5
  15.1 0.1 multiply_reduce_fusion.2
  15.3 0.6 copy-done.5
  15.8 0.1 fusion.57
  15.9 0.0 copy-done.13
  15.9 0.1 iota_compare_fusion
  16.0 0.5 add_rsqrt_fusion.1
  16.5 0.7 copy.46
  17.2 0.7 copy.45
  17.9 0.0 copy-done.3
  17.9 0.0 copy-done.7
  17.9 9.5 %multiply_reduce_fusion.1 = (f32[64]{0:T(128)S(1)}, f32[64,1536]{1,0:T(8,128)S(1)}) fusion(bf16[7168,1536]{1,0:T(8,128)(2,1)} %param.26, bf16[64,7168]{1,0:T(8,128)(2,1)S(1)} %copy-done.3, f32[7168]{0:T(1024)S(1)} %copy-done.7, f32[64]{0:T(128)S(1)} %add_rsqrt_fusion.3), kind=kOutput, calls=%fused_computation.46 | convolution fusion | flops 1411317760 | bytes 23360000 | tf_op jit(solution)/shard_map/dot_general | solution.py:29
  27.4 0.0 copy-done.15
  27.4 73.7 %fusion = f32[64,128,192]{1,0,2:T(8,128)} fusion(bf16[1536,128,192]{1,2,0:T(8,128)(2,1)} %param.28, f32[64,1536]{1,0:T(8,128)S(1)} %get-tuple-element.19, f32[1536]{0:T(1024)S(1)} %copy-done.15, f32[64]{0:T(128)S(1)} %add_rsqrt_fusion.2), kind=kOutput, calls=%fused_computation | convolution fusion | flops 4832133120 | bytes 82188544 | tf_op jit(solution)/shard_map/bl,lhe->bhe/dot_general | solution.py:30
  101.0 4.0 slice.44
  105.1 2.6 subtract_convert_fusion
  107.7 0.8 subtract_convert_fusion.1
  108.5 0.6 pad_maximum_fusion.1
  109.1 1.4 copy.41
  110.5 4.6 copy.32
  115.1 1.2 pad_maximum_fusion
  116.3 1.6 fusion.37
  117.8 0.0 copy-done
  117.8 4.6 fusion.39
  122.4 0.0 copy-done.6
  122.4 0.0 copy-done.11
  122.4 0.0 copy-done.12
  122.4 0.1 fusion.56
  122.5 0.0 copy-start.8
  122.5 25.2 %convert_bitcast_fusion = bf16[64,128,512]{2,0,1:T(8,128)(2,1)} fusion(bf16[64,128,128]{2,0,1:T(8,128)(2,1)} %copy.32, bf16[512,128,128]{2,1,0:T(8,128)(2,1)} %param.31), kind=kOutput, calls=%fused_computation.10 | convolution fusion | flops 1077936128 | bytes 27262976 | tf_op jit(solution)/shard_map/bhn,lhn->bhl/dot_general | solution.py:36
  147.8 0.0 copy-start.2
  147.8 0.0 copy-done.8
  147.8 8.1 %fusion.12 = f32[64,1,128]{2,1,0:T(1,128)S(1)} fusion(bf16[64,128,512]{2,0,1:T(8,128)(2,1)} %convert_bitcast_fusion, bf16[64,512,1]{1,0,2:T(8,128)(2,1)S(1)} %bitcast.55), kind=kOutput, calls=%fused_computation.17 | convolution fusion | flops 8388608 | bytes 8486912 | tf_op jit(solution)/shard_map/bhl,bl->bh/dot_general | solution.py:41
  155.9 0.0 copy-done.2
  155.9 19.9 %fusion.22 = (f32[64,128]{1,0:T(8,128)S(1)}, f32[64,128,256]{2,1,0:T(8,128)}) fusion(f32[64,128,256]{2,1,0:T(8,128)S(1)} %copy-done.2, pred[64,256]{1,0:T(8,128)(4,1)S(1)} %iota_compare_fusion, bf16[64,256,512]{2,1,0:T(8,128)(2,1)} %param.20, bf16[64,128,512]{2,0,1:T(8,128)(2,1)} %convert_bitcast_fusion), kind=kOutput, calls=%fused_computation.26 | convolution fusion | flops 2155864064 | bytes 41992192 | tf_op jit(solution)/shard_map/bhl,btl->bht/dot_general | solution.py:37
  175.7 5.5 fusion.10
  181.3 17.0 %divide_convert_fusion = bf16[64,128,512]{2,1,0:T(8,128)(2,1)} fusion(f32[64,128]{1,0:T(8,128)S(1)} %get-tuple-element.13, f32[64,512]{1,0:T(8,128)S(1)} %get-tuple-element.6, f32[64,128]{1,0:T(8,128)S(1)} %get-tuple-element.12, bf16[64,256,512]{2,1,0:T(8,128)(2,1)} %param.20, f32[64,128]{1,0:T(8,128)S(1)} %fusion.50, ...), kind=kOutput, calls=%fused_computation.6 | convolution fusion | flops 2174746624 | bytes 42188800 | tf_op jit(solution)/shard_map/bht,btl->bhl/dot_general | solution.py:47
  198.3 50.9 %fusion.24.clone.4 = bf16[64,128,128]{2,0,1:T(8,128)(2,1)} fusion(bf16[512,128,128]{2,1,0:T(8,128)(2,1)} %param.32, bf16[64,128,512]{2,1,0:T(8,128)(2,1)} %divide_convert_fusion), kind=kOutput, calls=%fused_computation.30.clone.clone.clone.1 | convolution fusion | flops 1074790400 | bytes 27262976 | tf_op jit(solution)/shard_map/bhl,lhv->bhv/dot_general | solution.py:50
  249.3 0.0 copy-start.10
  249.3 72.0 %multiply_reduce_fusion = (f32[64]{0:T(128)S(1)}, f32[64,7168]{1,0:T(8,128)S(1)}) fusion(bf16[128,128,7168]{2,1,0:T(8,128)(2,1)} %param.33, bf16[64,7168]{1,0:T(8,128)(2,1)S(1)} %copy-done.3, bf16[64,128,128]{2,0,1:T(8,128)(2,1)} %fusion.24.clone.4), kind=kOutput, calls=%fused_computation.37 | convolution fusion | flops 15035138048 | bytes 239730944 | tf_op jit(solution)/shard_map/bhv,hvd->bd/dot_general | solution.py:51
  321.3 0.0 copy-start.4
  321.3 0.0 copy-done.10
  321.3 1.4 multiply_convert_fusion
  322.7 0.0 all-gather.2.cloned.1.call-update
  322.7 0.0 reduce-scatter.2.cloned.1.call-start
  322.7 49.0 %all-gather.2.cloned.1.call-done = bf16[512,7168]{1,0:T(8,128)(2,1)} async-done(((bf16[64,7168]{1,0:T(8,128)(2,1)}), bf16[512,7168]{1,0:T(8,128)(2,1)}) %all-gather.2.cloned.1.call-update) | async-done | bytes 7340048 | tf_op jit(solution)/shard_map/all_gather | solution.py:67
  371.7 27.3 %fusion.62 = f32[512,2304]{1,0:T(8,128)S(1)} fusion(bf16[512,7168]{1,0:T(8,128)(2,1)} %all-gather.2.cloned.1.call-done, bf16[7168,2304]{1,0:T(8,128)(2,1)} %param.35), kind=kOutput, calls=%fused_computation.74 | convolution fusion | flops 16911433728 | bytes 45088768 | tf_op jit(solution)/shard_map/dot_general | solution.py:68
  399.0 0.0 copy-done.4
  399.1 0.0 copy-done.14
  399.1 23.5 %fusion.18.clone.4 = bf16[512,2304]{1,0:T(8,128)(2,1)} fusion(bf16[512,7168]{1,0:T(8,128)(2,1)S(1)} %copy-done.14, bf16[7168,2304]{1,0:T(8,128)(2,1)} %param.36, f32[512,2304]{1,0:T(8,128)S(1)} %fusion.62), kind=kOutput, calls=%fused_computation.22.clone.clone.clone.1 | convolution fusion | flops 16918511616 | bytes 47448064 | tf_op jit(solution)/shard_map/dot_general | solution.py:69
  422.6 27.0 %fusion.19 = f32[512,7168]{1,0:T(8,128)} fusion(bf16[2304,7168]{1,0:T(8,128)(2,1)} %param.37, bf16[512,2304]{1,0:T(8,128)(2,1)} %fusion.18.clone.4), kind=kOutput, calls=%fused_computation.23 | convolution fusion | flops 16911433728 | bytes 50069504 | tf_op jit(solution)/shard_map/dot_general | solution.py:71
  449.6 0.0 reduce-scatter.2.cloned.1.call-update
  449.6 0.7 copy-done.9
  450.3 0.7 copy.38
  451.0 97.8 %reduce-scatter.2.cloned.1.call-done = f32[64,7168]{1,0:T(8,128)} async-done(((f32[512,7168]{1,0:T(8,128)}), f32[64,7168]{1,0:T(8,128)}) %reduce-scatter.2.cloned.1.call-update) | async-done | bytes 1835024 | tf_op jit(solution)/shard_map/reduce_scatter | solution.py:72
  548.8 3.1 add_convert_fusion
  551.9 0.0 copy-done.1
  (12 shorter events, 0.1 us)
Async XLA Ops:
  7.2 110.7 %copy-start = (bf16[64,256,64]{1,2,0:T(8,128)(2,1)S(1)}, bf16[64,256,64]{1,2,0:T(8,128)(2,1)}, u32[]{:S(2)}) copy-start(bf16[64,256,64]{1,2,0:T(8,128)(2,1)} %param.21) | copy-start | bytes 6291460
  7.2 10.7 %copy-start.3 = (bf16[64,7168]{1,0:T(8,128)(2,1)S(1)}, bf16[64,7168]{1,0:T(8,128)(2,1)}, u32[]{:S(2)}) copy-start(bf16[64,7168]{1,0:T(8,128)(2,1)} %param.19) | copy-start | bytes 2752516
  7.2 10.7 %copy-start.7 = (f32[7168]{0:T(1024)S(1)}, f32[7168]{0:T(1024)}, u32[]{:S(2)}) copy-start(f32[7168]{0:T(1024)} %param.25) | copy-start | bytes 86020
  7.2 8.7 %copy-start.13 = (s32[64]{0:T(128)S(1)}, s32[64]{0:T(128)}, u32[]{:S(2)}) copy-start(s32[64]{0:T(128)} %param.22) | copy-start | bytes 772
  7.2 364.5 %all-gather.2.cloned.1.call-start = ((), (), s32[]{:S(2)}) async-start(), calls=%async_computation.1 | async-start | bytes 8257536 | tf_op jit(solution)/shard_map/all_gather | solution.py:67
  15.1 0.7 copy-start.5
  17.9 9.5 %copy-start.15 = (f32[1536]{0:T(1024)S(1)}, f32[1536]{0:T(1024)}, u32[]{:S(2)}) copy-start(f32[1536]{0:T(1024)} %param.27) | copy-start | bytes 18436
  115.1 7.3 %copy-start.6 = (f32[64,576]{1,0:T(8,128)S(1)}, f32[64,576]{1,0:T(8,128)}, u32[]{:S(2)}) copy-start(f32[64,576]{1,0:T(8,128)} %copy-done.5) | copy-start | bytes 442372
  115.1 7.3 %copy-start.11 = (f32[512]{0:T(512)S(1)}, f32[512]{0:T(512)}, u32[]{:S(2)}) copy-start(f32[512]{0:T(512)} %param.30) | copy-start | bytes 6148
  115.1 7.3 %copy-start.12 = (f32[64]{0:T(128)S(1)}, f32[64]{0:T(128)}, u32[]{:S(2)}) copy-start(f32[64]{0:T(128)} %add_rsqrt_fusion.1) | copy-start | bytes 772
  122.5 25.3 %copy-start.8 = (bf16[64,512]{1,0:T(8,128)(2,1)}, bf16[64,512]{1,0:T(8,128)(2,1)S(1)}, u32[]{:S(2)}) copy-start(bf16[64,512]{1,0:T(8,128)(2,1)S(1)} %get-tuple-element.7) | copy-start | bytes 196612
  147.8 8.1 %copy-start.2 = (f32[64,128,256]{2,1,0:T(8,128)S(1)}, f32[64,128,256]{2,1,0:T(8,128)}, u32[]{:S(2)}) copy-start(f32[64,128,256]{2,1,0:T(8,128)} %fusion.39) | copy-start | bytes 25165828
  249.3 72.0 %copy-start.10 = (f32[7168]{0:T(1024)S(1)}, f32[7168]{0:T(1024)}, u32[]{:S(2)}) copy-start(f32[7168]{0:T(1024)} %param.34) | copy-start | bytes 86020
  321.3 77.8 %copy-start.4 = (f32[64,7168]{1,0:T(8,128)}, f32[64,7168]{1,0:T(8,128)S(1)}, u32[]{:S(2)}) copy-start(f32[64,7168]{1,0:T(8,128)S(1)} %get-tuple-element.23) | copy-start | bytes 5505028
  322.7 226.1 %reduce-scatter.2.cloned.1.call-start = ((), (), s32[]{:S(2)}) async-start(), calls=%async_computation.2 | async-start | bytes 16515072 | tf_op jit(solution)/shard_map/reduce_scatter | solution.py:72
  371.7 27.3 %copy-start.14 = (bf16[512,7168]{1,0:T(8,128)(2,1)S(1)}, bf16[512,7168]{1,0:T(8,128)(2,1)}, u32[]{:S(2)}) copy-start(bf16[512,7168]{1,0:T(8,128)(2,1)} %all-gather.2.cloned.1.call-done) | copy-start | bytes 22020100
  449.6 0.7 copy-start.9
  449.6 102.3 %copy-start.1 = (bf16[64,256,64]{1,2,0:T(8,128)(2,1)S(1)}, bf16[64,256,64]{1,2,0:T(8,128)(2,1)}, u32[]{:S(2)}) copy-start(bf16[64,256,64]{1,2,0:T(8,128)(2,1)} %param.21) | copy-start | bytes 6291460
Sparse Core Ops, SparseCore 0:
  322.8 48.8 all-gather.1
  449.8 98.9 reduce-scatter.1
where the time goes:
time: 563 us; the launch traced here: 559 us
  matrix products  366 us (65%)
  waiting for transfers between devices  147 us (26%)
  other arithmetic  17.7 us (3%)
  between operations  14.5 us (3%)
  local copies, waits for them, and re-layouts  13.5 us (2%)
    reduce_scatter x1, waiting for transfers between devices, local_step(): lax.psum_scatter(partial_sum, 'dp', scatter_dimension=0, tiled=True)  97.8 us
    dot_general x1, matrix products, attention_rows(): jnp.einsum('bl,lhe->bhe', q_latent, w_uq, preferred_element_type=jnp.floa...  73.7 us
    dot_general x1, matrix products, attention_rows(): jnp.einsum('bhv,hvd->bd', head_out, w_out, preferred_element_type=jnp.flo...  72 us
    dot_general x1, matrix products, attention_rows(): jnp.einsum('bhl,lhv->bhv', lat_out, w_uv, preferred_element_type=jnp.floa...  50.9 us
    all_gather x1, waiting for transfers between devices, local_step(): group_in = lax.all_gather(mlp_in, 'dp', axis=0, tiled=True)  49 us
    dot_general x1, matrix products, local_step(): gate_val = jnp.dot(group_in, w_gate, preferred_element_type=jnp.float32)  27.3 us
    dot_general x1, matrix products, local_step(): partial_sum = jnp.dot(act_val, w_down, preferred_element_type=jnp.float32)  27 us
    dot_general x1, matrix products, attention_rows(): jnp.einsum('bhn,lhn->bhl', q_nope, w_uk, preferred_element_type=jnp.float32)  25.2 us
  transfers between devices with their start and end apart: 2, of which 2 were waited for; matrix products, arithmetic and copies ran while one was open for 0% of the time, Pallas kernels for 0%

commit v1 on v0

v1 whole, which is shorter than its diff:
```python
import functools
import math
import jax
import jax.numpy as jnp
from jax import lax
from jax.experimental import pallas as pl
from jax.experimental.pallas import tpu as pltpu
from jax.sharding import PartitionSpec as P

BF = jnp.bfloat16
F32 = jnp.float32
QS = 200
HS = 72
LC = 256


def start_rows(w_hbm, buf, sem, l0, count):
    def one(l, _):
        pltpu.make_async_copy(w_hbm.at[l0 + l], buf.at[:, pl.ds(pl.multiple_of(2 * l, 2), 2), :], sem).start()
        return 0
    lax.fori_loop(0, count, one, 0, unroll=8)


def spread(par):
    rows = lax.broadcasted_iota(jnp.int32, (128, 256), 0)
    cols = lax.broadcasted_iota(jnp.int32, (128, 256), 1)
    return jnp.where(cols == 2 * rows + par, 1.0, 0.0).astype(BF)


def uq_kernel(cq_ref, cos_ref, sin_ref, w_hbm, qn_ref, qr_ref, buf, acc, a2, q_scr, h_scr, sems):
    n_chunk = w_hbm.shape[0] // LC
    B = cq_ref.shape[0]
    P = w_hbm.shape[1]
    start_rows(w_hbm, buf.at[0], sems.at[0], 0, LC)
    for par in range(2):
        x = spread(par)
        for k in range(cq_ref.shape[1] // 128):
            a2[par * B:(par + 1) * B, k * 256:(k + 1) * 256] = jnp.dot(
                cq_ref[:, k * 128:(k + 1) * 128], x, preferred_element_type=F32).astype(BF)
    for c in range(n_chunk):
        slot = c % 2
        if c + 1 < n_chunk:
            start_rows(w_hbm, buf.at[1 - slot], sems.at[1 - slot], (c + 1) * LC, LC)
        pltpu.make_async_copy(buf.at[slot], buf.at[slot], sems.at[slot]).wait()
        lhs = a2[:, c * 2 * LC:(c + 1) * 2 * LC]

        def body(j, _):
            rhs = jnp.concatenate([buf[slot, 2 * j], buf[slot, 2 * j + 1]], axis=1)
            out = jnp.dot(lhs, rhs, preferred_element_type=F32)
            r0 = pl.multiple_of(j * 2 * B, 2 * B)
            if c > 0:
                out = out + acc[pl.ds(r0, 2 * B), :]
            if c < n_chunk - 1:
                acc[pl.ds(r0, 2 * B), :] = out
            else:
                for half in range(2):
                    for par in range(2):
                        q_scr[pl.ds(4 * j + 2 * half + par, B, stride=QS), :] = out[par * B:(par + 1) * B, half * 128:(half + 1) * 128]
            return 0
        lax.fori_loop(0, P // 2, body, 0, unroll=8)

    def tb(b, _):
        blk = q_scr[pl.ds(pl.multiple_of(b * QS, 8), 192), :]
        h_scr[pl.ds(b, 128, stride=HS), :] = blk[:128].T
        v = blk[128:192].T
        rot = jnp.concatenate([v[:, 32:], v[:, :32]], axis=1)
        qr_ref[b] = (v * cos_ref[pl.ds(b, 1), :] + rot * sin_ref[pl.ds(b, 1), :]).astype(BF)
        return 0
    lax.fori_loop(0, B, tb, 0, unroll=2)

    def hb(h, _):
        qn_ref[h] = h_scr[pl.ds(pl.multiple_of(h * HS, 8), B), :].astype(BF)
        return 0
    lax.fori_loop(0, 128, hb, 0, unroll=8)


def uq(cq, w_uq, cos2, sin2):
    B, L = cq.shape
    w4 = w_uq.transpose(0, 2, 1).reshape(L, 96, 2, 128)
    vm = pl.BlockSpec(memory_space=pltpu.VMEM)
    return pl.pallas_call(
        uq_kernel,
        in_specs=[vm, vm, vm, pl.BlockSpec(memory_space=pl.ANY)],
        out_specs=[vm, vm],
        out_shape=[jax.ShapeDtypeStruct((128, B, 128), BF), jax.ShapeDtypeStruct((B, 128, 64), BF)],
        scratch_shapes=[pltpu.VMEM((2, 96, 2 * LC, 128), BF), pltpu.VMEM((96 * B, 256), F32), pltpu.VMEM((2 * B, 2 * L), BF),
                        pltpu.VMEM((B * QS, 128), F32), pltpu.VMEM((128 * HS, 128), F32), pltpu.SemaphoreType.DMA((2,))],
        compiler_params=pltpu.CompilerParams(vmem_limit_bytes=60 * 1024 * 1024),
        cost_estimate=pl.CostEstimate(flops=2 * B * L * 24576, bytes_accessed=76 * 10**6, transcendentals=0),
        name="uq",
    )(cq, cos2, sin2, w4)


UL = 128
KS = 136


def uk_kernel(qn_ref, w_hbm, ql_ref, buf, scr, sel, sems):
    B = qn_ref.shape[1]
    n_chunk = w_hbm.shape[0] // UL
    P = w_hbm.shape[1]
    start_rows(w_hbm, buf.at[0], sems.at[0], 0, UL)
    sel[0:128] = spread(0)
    sel[128:256] = spread(1)
    for c in range(n_chunk):
        slot = c % 2
        if c + 1 < n_chunk:
            start_rows(w_hbm, buf.at[1 - slot], sems.at[1 - slot], (c + 1) * UL, UL)
        pltpu.make_async_copy(buf.at[slot], buf.at[slot], sems.at[slot]).wait()

        def body(j, _):
            rhs = jnp.concatenate([buf[slot, 2 * j], buf[slot, 2 * j + 1]], axis=1)
            w = jnp.dot(sel[...], rhs, preferred_element_type=F32).astype(BF)
            for half in range(2):
                for par in range(2):
                    h = 4 * j + 2 * half + par
                    out = lax.dot_general(qn_ref[h], w[par * UL:(par + 1) * UL, half * 128:(half + 1) * 128],
                                          (((1,), (1,)), ((), ())), preferred_element_type=F32)
                    scr[pl.ds(h, B, stride=KS), :] = out
            return 0
        lax.fori_loop(0, P // 2, body, 0, unroll=4)

        def cb(b, _):
            ql_ref[b, :, c * UL:(c + 1) * UL] = scr[pl.ds(pl.multiple_of(b * KS, 8), 128), :].astype(BF)
            return 0
        lax.fori_loop(0, B, cb, 0, unroll=4)


def uk(qn, w_uk):
    B = qn.shape[1]
    vm = pl.BlockSpec(memory_space=pltpu.VMEM)
    return pl.pallas_call(
        uk_kernel,
        in_specs=[vm, pl.BlockSpec(memory_space=pl.ANY)],
        out_specs=vm,
        out_shape=jax.ShapeDtypeStruct((B, 128, 512), BF),
        scratch_shapes=[pltpu.VMEM((2, 64, 2 * UL, 128), BF), pltpu.VMEM((B * KS, 128), F32), pltpu.VMEM((256, 256), BF),
                        pltpu.SemaphoreType.DMA((2,))],
        compiler_params=pltpu.CompilerParams(vmem_limit_bytes=60 * 1024 * 1024),
        cost_estimate=pl.CostEstimate(flops=2 * B * 128 * 128 * 512, bytes_accessed=26 * 10**6, transcendentals=0),
        name="uk",
    )(qn, w_uk.reshape(512, 64, 2, 128))


NB = 4


def attn_kernel(scale, len_ref, ql_ref, qr_ref, ckv_ref, kpe_ref, cn_ref, kn_ref, ol_ref):
    T = ckv_ref.shape[1]
    dn = (((1,), (1,)), ((), ()))
    for i in range(NB):
        pos = len_ref[pl.program_id(0) * NB + i]
        row = lax.broadcasted_iota(jnp.int32, ckv_ref.shape[1:], 0)
        ckv = jnp.where(row == pos, cn_ref[i], ckv_ref[i])
        lane = lax.broadcasted_iota(jnp.int32, (128, T), 1)
        kn = jnp.broadcast_to(kn_ref[i], (T, 64))
        s_new = lax.dot_general(qr_ref[i], kn, dn, preferred_element_type=F32)
        s_pe = jnp.dot(qr_ref[i], kpe_ref[i], preferred_element_type=F32)
        s = lax.dot_general(ql_ref[i], ckv, dn, preferred_element_type=F32)
        s = (s + jnp.where(lane == pos, s_new, s_pe)) * scale
        s = jnp.where(lane <= pos, s, -jnp.inf)
        e = jnp.exp(s - jnp.max(s, axis=1, keepdims=True))
        den = jnp.sum(e, axis=1, keepdims=True)
        ol = jnp.dot(e.astype(BF), ckv, preferred_element_type=F32)
        ol = (ol / den).astype(BF)
        for k in range(4):
            ol_ref[i, k] = ol[:, k * 128:(k + 1) * 128]


def attn(scale, length, ql, qr, ckv, kpe, c_new, k_new):
    B, T, L = ckv.shape
    spec = lambda *s: pl.BlockSpec((NB,) + s, lambda i, _: (i, 0, 0))
    return pl.pallas_call(
        functools.partial(attn_kernel, scale),
        grid_spec=pltpu.PrefetchScalarGridSpec(
            num_scalar_prefetch=1, grid=(B // NB,),
            in_specs=[spec(128, L), spec(128, 64), spec(T, L), spec(64, T), spec(1, L), spec(1, 64)],
            out_specs=pl.BlockSpec((NB, 4, 128, 128), lambda i, _: (i, 0, 0, 0))),
        out_shape=jax.ShapeDtypeStruct((B, 4, 128, 128), BF),
        compiler_params=pltpu.CompilerParams(vmem_limit_bytes=40 * 2**20),
        cost_estimate=pl.CostEstimate(flops=2 * B * 128 * T * 1100, bytes_accessed=40 * 10**6, transcendentals=B * 128 * T),
        name="attn",
    )(length, ql, qr, ckv, kpe.transpose(0, 2, 1), c_new.reshape(B, 1, L), k_new.reshape(B, 1, 64))


VP = 16


def uv_kernel(ol_hbm, w_hbm, o_ref, wbuf, abuf, sel, wsems, asem):
    B = ol_hbm.shape[0]
    n_chunk = 64 // VP

    def start_w(c, slot):
        def one(l, _):
            pltpu.make_async_copy(w_hbm.at[l, pl.ds(c * VP, VP)], wbuf.at[slot, :, pl.ds(pl.multiple_of(2 * l, 2), 2), :], wsems.at[slot]).start()
            return 0
        lax.fori_loop(0, 512, one, 0, unroll=8)
    def start_a(b, _):
        pltpu.make_async_copy(ol_hbm.at[b], abuf.at[:, :, pl.ds(pl.multiple_of(2 * b, 2), 2), :], asem).start()
        return 0
    lax.fori_loop(0, B, start_a, 0, unroll=8)
    start_w(0, 0)
    sel[0:128] = spread(0)
    sel[128:256] = spread(1)
    half_rows = lax.broadcasted_iota(jnp.int32, (2 * B, 2 * B), 0)
    half_cols = lax.broadcasted_iota(jnp.int32, (2 * B, 2 * B), 1)
    want = jnp.where(half_rows < B, 2 * half_rows, 2 * (half_rows - B) + 1)
    pick = jnp.where(half_cols == want, 1.0, 0.0).astype(BF)
    pltpu.make_async_copy(abuf, abuf, asem).wait()
    for c in range(n_chunk):
        slot = c % 2
        if c + 1 < n_chunk:
            start_w(c + 1, 1 - slot)
        pltpu.make_async_copy(wbuf.at[slot], wbuf.at[slot], wsems.at[slot]).wait()

        def body(j, _):
            p = c * VP + 2 * j
            out = [None, None]
            for k in range(4):
                rhs = jnp.concatenate([wbuf[slot, 2 * j, k * 256:(k + 1) * 256], wbuf[slot, 2 * j + 1, k * 256:(k + 1) * 256]], axis=1)
                w = jnp.dot(sel[...], rhs, preferred_element_type=F32).astype(BF)
                for half in range(2):
                    wh = w[:, half * 128:(half + 1) * 128]
                    wk = jnp.concatenate([wh[0:128], wh[128:256]], axis=1)
                    part = jnp.dot(abuf[k, p + half], wk, preferred_element_type=F32)
                    out[half] = part if out[half] is None else out[half] + part
            for half in range(2):
                r = jnp.dot(pick, out[half].astype(BF), preferred_element_type=F32).astype(BF)
                col = pl.multiple_of((p + half) * 256, 256)
                o_ref[:, pl.ds(col, 128)] = r[0:B, 0:128]
                o_ref[:, pl.ds(col + 128, 128)] = r[B:2 * B, 128:256]
            return 0
        lax.fori_loop(0, VP // 2, body, 0, unroll=2)


def uv(ol, w_uv):
    B = ol.shape[0]
    return pl.pallas_call(
        uv_kernel,
        in_specs=[pl.BlockSpec(memory_space=pl.ANY)] * 2,
        out_specs=pl.BlockSpec(memory_space=pltpu.VMEM),
        out_shape=jax.ShapeDtypeStruct((B, 128 * 128), BF),
        scratch_shapes=[pltpu.VMEM((2, VP, 1024, 128), BF), pltpu.VMEM((4, 64, 2 * B, 128), BF), pltpu.VMEM((256, 256), BF),
                        pltpu.SemaphoreType.DMA((2,)), pltpu.SemaphoreType.DMA],
        compiler_params=pltpu.CompilerParams(vmem_limit_bytes=60 * 1024 * 1024),
        cost_estimate=pl.CostEstimate(flops=2 * B * 128 * 128 * 512, bytes_accessed=26 * 10**6, transcendentals=0),
        name="uv",
    )(ol.reshape(B, 4, 64, 2, 128), w_uv.reshape(512, 64, 2, 128))

EPSILON = 1e-6
MSCALE = 0.1 * math.log(40.0) + 1.0


def rms_norm(values_in, gain_vec):
    floats = values_in.astype(jnp.float32)
    mean_sq = jnp.mean(floats * floats, axis=-1, keepdims=True)
    return floats * lax.rsqrt(mean_sq + EPSILON) * gain_vec


def apply_rope(values_in, cos_t, sin_t):
    half_dim = values_in.shape[-1] // 2
    low_half = values_in[..., :half_dim]
    high_half = values_in[..., half_dim:]
    return jnp.concatenate([low_half * cos_t - high_half * sin_t, high_half * cos_t + low_half * sin_t], axis=-1)


def attention_rows(hidden, ckv_cache, kpe_cache, cache_len, rope_cos, rope_sin, norm_attn, w_dq, norm_q, w_uq, w_dkv, norm_kv, w_uk, w_uv, w_out):
    value_dim = w_uk.shape[0]
    score_scale = MSCALE * MSCALE / math.sqrt(w_uq.shape[2])
    normed = rms_norm(hidden, norm_attn).astype(BF)
    q_latent = rms_norm(jnp.dot(normed, w_dq, preferred_element_type=jnp.float32), norm_q).astype(BF)
    kv_full = jnp.dot(normed, w_dkv, preferred_element_type=jnp.float32)
    ckv_new = rms_norm(kv_full[:, :value_dim], norm_kv).astype(BF)
    kpe_new = apply_rope(kv_full[:, value_dim:], rope_cos, rope_sin).astype(BF)
    qn, qr = uq(q_latent, w_uq, jnp.concatenate([rope_cos, rope_cos], axis=1), jnp.concatenate([-rope_sin, rope_sin], axis=1))
    ql = uk(qn, w_uk)
    ol = attn(score_scale, cache_len, ql, qr, ckv_cache, kpe_cache, ckv_new, kpe_new)
    head_out = uv(ol, w_uv)
    attn_out = jnp.dot(head_out, w_out.reshape(-1, w_out.shape[2]), preferred_element_type=jnp.float32)
    residual = (hidden.astype(jnp.float32) + attn_out).astype(BF)
    return residual, ckv_new, kpe_new


def solution(mesh):
    row_spec = P(('rep', 'dp'), None)
    cube_spec = P(('rep', 'dp'), None, None)
    full_spec = P()
    in_specs = (row_spec, cube_spec, cube_spec, P(('rep', 'dp')), row_spec, row_spec,
                full_spec, full_spec, full_spec, full_spec, full_spec, full_spec, full_spec, full_spec, full_spec, full_spec,
                P(None, 'dp'), P(None, 'dp'), P('dp', None))

    def local_step(hidden, ckv_cache, kpe_cache, cache_len, rope_cos, rope_sin, norm_attn, w_dq, norm_q, w_uq, w_dkv, norm_kv, w_uk, w_uv, w_out, norm_mlp, w_gate, w_up, w_down):
        residual, ckv_new, kpe_new = attention_rows(hidden, ckv_cache, kpe_cache, cache_len, rope_cos, rope_sin, norm_attn, w_dq, norm_q, w_uq, w_dkv, norm_kv, w_uk, w_uv, w_out)
        mlp_in = rms_norm(residual, norm_mlp).astype(jnp.bfloat16)
        group_in = lax.all_gather(mlp_in, 'dp', axis=0, tiled=True)
        gate_val = jnp.dot(group_in, w_gate, preferred_element_type=jnp.float32)
        up_val = jnp.dot(group_in, w_up, preferred_element_type=jnp.float32)
        act_val = (jax.nn.silu(gate_val) * up_val).astype(jnp.bfloat16)
        partial_sum = jnp.dot(act_val, w_down, preferred_element_type=jnp.float32)
        mlp_rows = lax.psum_scatter(partial_sum, 'dp', scatter_dimension=0, tiled=True)
        out_hidden = (residual.astype(jnp.float32) + mlp_rows).astype(jnp.bfloat16)
        return out_hidden, ckv_new, kpe_new

    return jax.shard_map(local_step, mesh=mesh, in_specs=in_specs, out_specs=(row_spec, row_spec, row_spec), check_vma=False)
```

time: 563 us -> 490 us (0.87)
  matrix products: 366 us -> 166 us
  Pallas kernels: 0 us -> 148 us
  other arithmetic: 17.7 us -> 7.77 us
  local copies, waits for them, and re-layouts: 13.5 us -> 7.42 us
    dot_general x9 -> x1, matrix products: 273 us -> 72 us  [attention_rows(): jnp.dot(head_out, w_out.reshape(-1, w_out.shape[2]), preferred_element_ty...]
    pallas_call x0 -> x4, Pallas kernels: none -> 148 us  [the longest x1 43.3 us: uv(): pl.pallas_call(uv_kernel, in_specs=[pl.BlockSpec(memory_space=pl.ANY)] *...]
    slice x2 -> x0, local copies, waits for them, and re-layouts: 8.61 us -> none  [attention_rows(): q_nope = q_full[..., :nope_dim].astype(jnp.bfloat16)]
where the time goes in v1:
time: 490 us
  matrix products  166 us (34%)
  Pallas kernels  148 us (30%)
  waiting for transfers between devices  146 us (30%)
  between operations  14.4 us (3%)
  other arithmetic  7.77 us (2%)
  local copies, waits for them, and re-layouts  7.42 us (2%)
    reduce_scatter x1, waiting for transfers between devices, local_step(): lax.psum_scatter(partial_sum, 'dp', scatter_dimension=0, tiled=True)  97.1 us
    dot_general x1, matrix products, attention_rows(): jnp.dot(head_out, w_out.reshape(-1, w_out.shape[2]), preferred_element_ty...  72 us
    all_gather x1, waiting for transfers between devices, local_step(): group_in = lax.all_gather(mlp_in, 'dp', axis=0, tiled=True)  49 us
    pallas_call x1, Pallas kernels, uv(): pl.pallas_call(uv_kernel, in_specs=[pl.BlockSpec(memory_space=pl.ANY)] *...  43.3 us
    pallas_call x1, Pallas kernels, uk(): pl.pallas_call(uk_kernel, in_specs=[vm, pl.BlockSpec(memory_space=pl.ANY)...  41.3 us
    pallas_call x1, Pallas kernels, uq(): pl.pallas_call(uq_kernel, in_specs=[vm, vm, vm, pl.BlockSpec(memory_space...  37.5 us
    dot_general x1, matrix products, local_step(): gate_val = jnp.dot(group_in, w_gate, preferred_element_type=jnp.float32)  27.3 us
    dot_general x1, matrix products, local_step(): partial_sum = jnp.dot(act_val, w_down, preferred_element_type=jnp.float32)  26.9 us
  transfers between devices with their start and end apart: 2, of which 2 were waited for; matrix products, arithmetic and copies ran while one was open for 0% of the time, Pallas kernels for 0%

profile of v1, /device:TPU:0, one launch (start us, length us, event | category | flops | bytes accessed | tf_op | source)
XLA Modules:
  0.0 489.8 jit_solution(10484707203172859601)
XLA Ops:
  7.2 0.0 all-gather.2.cloned.1.call-start
  7.2 1.5 fusion.5
  8.7 0.0 copy-start.12
  8.7 0.0 copy-start.13
  8.7 0.0 copy-start.16
  8.7 0.0 copy-start.4
  8.7 0.0 copy-start.7
  8.7 6.3 %fusion.8 = f32[64,576]{1,0:T(8,128)S(1)} fusion(bf16[7168,576]{0,1:T(8,128)(2,1)} %param.29, bf16[64,7168]{1,0:T(8,128)(2,1)} %param.19, f32[7168]{0:T(1024)} %param.25, f32[64]{0:T(128)S(1)} %add_rsqrt_fusion.3), kind=kOutput, calls=%fused_computation.17 | convolution fusion | flops 530317312 | bytes 9351424 | tf_op jit(solution)/shard_map/dot_general | solution.py:272
  15.0 0.0 copy-start.5
  15.1 0.1 multiply_reduce_fusion.2
  15.2 0.1 fusion.13
  15.2 0.0 copy-done.12
  15.2 0.1 copy.55
  15.3 0.0 copy-done.13
  15.3 0.1 copy.58
  15.4 0.0 copy-start.18
  15.4 0.1 copy.66
  15.5 0.1 copy.65
  15.6 0.0 copy-start.10
  15.6 0.0 copy-start.8
  15.6 0.1 copy.57
  15.7 0.1 copy.62
  15.8 0.4 copy-done.10
  16.2 0.1 copy.61
  16.3 0.0 copy-done.16
  16.3 0.1 fusion.24
  16.4 0.1 copy.63.cn_ref
  16.5 0.0 copy-done.4
  16.5 0.0 copy-done.7
  16.5 0.0 copy-start.15
  16.5 9.6 %multiply_reduce_fusion.1 = (f32[64]{0:T(128)S(1)}, f32[64,1536]{1,0:T(8,128)S(1)}) fusion(bf16[7168,1536]{1,0:T(8,128)(2,1)} %param.26, bf16[64,7168]{1,0:T(8,128)(2,1)S(1)} %copy-done.4, f32[7168]{0:T(1024)S(1)} %copy-done.7, f32[64]{0:T(128)S(1)} %add_rsqrt_fusion.3), kind=kOutput, calls=%fused_computation.16 | convolution fusion | flops 1411317760 | bytes 23360000 | tf_op jit(solution)/shard_map/dot_general | solution.py:271
  26.2 0.0 copy-done.5
  26.2 0.1 pad_maximum_fusion.2.kn_ref
  26.4 0.7 pad_maximum_fusion
  27.1 0.8 multiply_convert_fusion.1.cq_ref
  27.8 37.5 %uq.1 = (bf16[128,64,128]{2,1,0:T(8,128)(2,1)}, bf16[64,128,64]{2,1,0:T(8,128)(2,1)}) custom-call(bf16[64,1536]{1,0:T(8,128)(2,1)} %multiply_convert_fusion.1.cq_ref, f32[64,64]{1,0:T(8,128)} %get-tuple-element.19.cos_ref, f32[64,64]{1,0:T(8,128)} %get-tuple-element.20.sin_ref, bf16[1536,96,2,128]{3,2,1,0:T(2,128)(2,1)} %bitcast.1.w_hbm), custom_call_target="tpu_custom_call" | custom-call | flops 4831838208 | bytes 76000000 | tf_op jit(solution)/shard_map/uq/pallas_call | solution.py:81
  65.4 0.0 copy-start.1
  65.4 0.0 copy-start.3
  65.4 41.3 %uk.1.ql_ref = bf16[64,128,512]{2,1,0:T(8,128)(2,1)} custom-call(bf16[128,64,128]{2,1,0:T(8,128)(2,1)} %get-tuple-element.5.qn_ref, bf16[512,64,2,128]{3,2,1,0:T(2,128)(2,1)} %bitcast.31), custom_call_target="tpu_custom_call" | custom-call | flops 1073741824 | bytes 26000000 | tf_op jit(solution)/shard_map/uk/pallas_call | solution.py:132
  106.7 1.6 copy-done.2
  108.3 26.3 %attn.1 = bf16[64,4,128,128]{3,2,1,0:T(8,128)(2,1)S(1)} custom-call(s32[64]{0:T(128)S(1)} %copy-done.3, bf16[64,128,512]{2,1,0:T(8,128)(2,1)} %uk.1.ql_ref, bf16[64,128,64]{2,1,0:T(8,128)(2,1)S(1)} %copy-done.2, bf16[64,256,512]{2,1,0:T(8,128)(2,1)} %ckv_ref.1, bf16[64,64,256]{2,1,0:T(8,128)(2,1)S(1)} %bitcast.30, bf16[64,1,512]{2,1,0:T(2,128)(2,1)S(1)} %copy.63.cn_ref, ...), custom_call_target="tpu_custom_call" | custom-call | flops 4613734400 | bytes 40000000 | tf_op jit(solution)/shard_map/attn/pallas_call | solution.py:173
  134.7 3.2 copy-done
  137.9 43.3 %uv.1 = bf16[64,16384]{1,0:T(8,128)(2,1)} custom-call(bf16[64,4,64,2,128]{4,3,2,1,0:T(2,128)(2,1)} %bitcast.29, bf16[512,64,2,128]{3,2,1,0:T(2,128)(2,1)} %bitcast.32), custom_call_target="tpu_custom_call" | custom-call | flops 1073741824 | bytes 26000000 | tf_op jit(solution)/shard_map/uv/pallas_call | solution.py:238
  181.1 0.0 copy-start.14
  181.2 72.0 %multiply_reduce_fusion = (f32[64]{0:T(128)S(1)}, f32[64,7168]{1,0:T(8,128)S(1)}) fusion(bf16[64,16384]{1,0:T(8,128)(2,1)} %uv.1, bf16[16384,7168]{1,0:T(8,128)(2,1)} %bitcast.9, bf16[64,7168]{1,0:T(8,128)(2,1)S(1)} %copy-done.4), kind=kOutput, calls=%fused_computation.14 | convolution fusion | flops 15035138048 | bytes 239730944 | tf_op jit(solution)/shard_map/dot_general | solution.py:279
  253.2 0.0 copy-done.14
  253.2 1.2 multiply_convert_fusion
  254.4 0.0 all-gather.2.cloned.1.call-update
  254.4 0.0 reduce-scatter.2.cloned.1.call-start
  254.4 49.0 %all-gather.2.cloned.1.call-done = bf16[512,7168]{1,0:T(8,128)(2,1)} async-done(((bf16[64,7168]{1,0:T(8,128)(2,1)}), bf16[512,7168]{1,0:T(8,128)(2,1)}) %all-gather.2.cloned.1.call-update) | async-done | bytes 7340048 | tf_op jit(solution)/shard_map/all_gather | solution.py:295
  303.4 27.3 %fusion.14 = f32[512,2304]{1,0:T(8,128)S(1)} fusion(bf16[512,7168]{1,0:T(8,128)(2,1)} %all-gather.2.cloned.1.call-done, bf16[7168,2304]{1,0:T(8,128)(2,1)} %param.35), kind=kOutput, calls=%fused_computation.33 | convolution fusion | flops 16911433728 | bytes 45088768 | tf_op jit(solution)/shard_map/dot_general | solution.py:296
  330.7 23.5 %fusion.2.clone.4 = bf16[512,2304]{1,0:T(8,128)(2,1)} fusion(bf16[512,7168]{1,0:T(8,128)(2,1)S(1)} %copy-done.20, bf16[7168,2304]{1,0:T(8,128)(2,1)} %param.36, f32[512,2304]{1,0:T(8,128)S(1)} %fusion.14), kind=kOutput, calls=%fused_computation.4.clone.clone.clone.1 | convolution fusion | flops 16918511616 | bytes 47448064 | tf_op jit(solution)/shard_map/dot_general | solution.py:297
  354.3 26.9 %fusion.3 = f32[512,7168]{1,0:T(8,128)} fusion(bf16[2304,7168]{1,0:T(8,128)(2,1)} %param.37, bf16[512,2304]{1,0:T(8,128)(2,1)} %fusion.2.clone.4), kind=kOutput, calls=%fused_computation.5 | convolution fusion | flops 16911433728 | bytes 50069504 | tf_op jit(solution)/shard_map/dot_general | solution.py:299
  381.1 0.0 copy-start.17
  381.1 0.0 copy-start.19
  381.2 0.0 reduce-scatter.2.cloned.1.call-update
  381.2 0.6 copy-done.9
  381.8 0.0 copy-done.11
  381.9 0.7 copy.64
  382.6 0.0 copy-done.6
  382.6 0.0 copy-done.19
  382.6 0.7 multiply_convert_fusion.2
  383.3 97.1 %reduce-scatter.2.cloned.1.call-done = f32[64,7168]{1,0:T(8,128)} async-done(((f32[512,7168]{1,0:T(8,128)}), f32[64,7168]{1,0:T(8,128)}) %reduce-scatter.2.cloned.1.call-update) | async-done | bytes 1835024 | tf_op jit(solution)/shard_map/reduce_scatter | solution.py:300
  480.4 2.6 add_convert_fusion
  (19 shorter events, 0.1 us)
Async XLA Ops:
  7.2 296.2 %all-gather.2.cloned.1.call-start = ((), (), s32[]{:S(2)}) async-start(), calls=%async_computation.1 | async-start | bytes 8257536 | tf_op jit(solution)/shard_map/all_gather | solution.py:295
  8.7 6.6 %copy-start.12 = (f32[64,32]{0,1:T(8,128)S(1)}, f32[64,32]{0,1:T(8,128)}, u32[]{:S(2)}) copy-start(f32[64,32]{0,1:T(8,128)} %param.23) | copy-start | bytes 24580
  8.7 6.6 %copy-start.13 = (f32[64,32]{0,1:T(8,128)S(1)}, f32[64,32]{0,1:T(8,128)}, u32[]{:S(2)}) copy-start(f32[64,32]{0,1:T(8,128)} %param.24) | copy-start | bytes 24580
  8.7 7.6 %copy-start.16 = (f32[512]{0:T(512)S(1)}, f32[512]{0:T(512)}, u32[]{:S(2)}) copy-start(f32[512]{0:T(512)} %param.30) | copy-start | bytes 6148
  8.7 7.8 %copy-start.4 = (bf16[64,7168]{1,0:T(8,128)(2,1)S(1)}, bf16[64,7168]{1,0:T(8,128)(2,1)}, u32[]{:S(2)}) copy-start(bf16[64,7168]{1,0:T(8,128)(2,1)} %param.19) | copy-start | bytes 2752516
  8.7 7.8 %copy-start.7 = (f32[7168]{0:T(1024)S(1)}, f32[7168]{0:T(1024)}, u32[]{:S(2)}) copy-start(f32[7168]{0:T(1024)} %param.25) | copy-start | bytes 86020
  15.0 11.2 %copy-start.5 = (f32[64,576]{1,0:T(8,128)}, f32[64,576]{1,0:T(8,128)S(1)}, u32[]{:S(2)}) copy-start(f32[64,576]{1,0:T(8,128)S(1)} %fusion.8) | copy-start | bytes 442372
  15.4 10.8 %copy-start.18 = (f32[64]{0:T(128)}, f32[64]{0:T(128)S(1)}, u32[]{:S(2)}) copy-start(f32[64]{0:T(128)S(1)} %add_rsqrt_fusion.1) | copy-start | bytes 772
  15.6 0.6 copy-start.10
  15.6 10.6 %copy-start.8 = (bf16[64,32]{0,1:T(8,128)(2,1)}, bf16[64,32]{0,1:T(8,128)(2,1)S(1)}, u32[]{:S(2)}) copy-start(bf16[64,32]{0,1:T(8,128)(2,1)S(1)} %get-tuple-element.12) | copy-start | bytes 12292
  16.5 10.5 %copy-start.15 = (f32[1536]{0:T(1024)S(1)}, f32[1536]{0:T(1024)}, u32[]{:S(2)}) copy-start(f32[1536]{0:T(1024)} %param.27) | copy-start | bytes 18436
  65.4 41.3 %copy-start.1 = (bf16[64,256,64]{1,2,0:T(8,128)(2,1)S(1)}, bf16[64,256,64]{1,2,0:T(8,128)(2,1)}, u32[]{:S(2)}) copy-start(bf16[64,256,64]{1,2,0:T(8,128)(2,1)} %param.21) | copy-start | bytes 6291460
  65.4 41.3 %copy-start.3 = (s32[64]{0:T(128)S(1)}, s32[64]{0:T(128)}, u32[]{:S(2)}) copy-start(s32[64]{0:T(128)} %len_ref.1) | copy-start | bytes 772
  106.7 1.6 copy-start.2
  134.6 3.2 copy-start
  181.1 72.0 %copy-start.14 = (f32[7168]{0:T(1024)S(1)}, f32[7168]{0:T(1024)}, u32[]{:S(2)}) copy-start(f32[7168]{0:T(1024)} %param.34) | copy-start | bytes 86020
  254.4 226.0 %reduce-scatter.2.cloned.1.call-start = ((), (), s32[]{:S(2)}) async-start(), calls=%async_computation.2 | async-start | bytes 16515072 | tf_op jit(solution)/shard_map/reduce_scatter | solution.py:300
  303.4 27.3 %copy-start.20 = (bf16[512,7168]{1,0:T(8,128)(2,1)S(1)}, bf16[512,7168]{1,0:T(8,128)(2,1)}, u32[]{:S(2)}) copy-start(bf16[512,7168]{1,0:T(8,128)(2,1)} %all-gather.2.cloned.1.call-done) | copy-start | bytes 22020100
  381.1 0.7 copy-start.9
  381.1 0.7 copy-start.11
  381.1 1.4 copy-start.6
  381.1 1.4 copy-start.17
  381.1 1.4 copy-start.19
Sparse Core Ops, SparseCore 0:
  254.5 48.8 all-gather.1
  381.3 99.0 reduce-scatter.1

commit v2 on v1

v2 whole, which is shorter than its diff:
```python
import functools
import math
import jax
import jax.numpy as jnp
from jax import lax
from jax.experimental import pallas as pl
from jax.experimental.pallas import tpu as pltpu
from jax.sharding import PartitionSpec as P

EPSILON = 1e-6
MSCALE = 0.1 * math.log(40.0) + 1.0
BF = jnp.bfloat16
F32 = jnp.float32
LANES = 128
WIDE = 256
LATENT = 512
NT = (((1,), (1,)), ((), ()))
VMEM_BYTES = 60 * 1024 * 1024
QS = 200
HS = 72
LC = 256


def start_rows(w_hbm, buf, sem, l0, count):
    def one(l, _):
        pltpu.make_async_copy(w_hbm.at[l0 + l], buf.at[:, pl.ds(pl.multiple_of(2 * l, 2), 2), :], sem).start()
        return 0
    lax.fori_loop(0, count, one, 0, unroll=8)


def spread(par):
    rows = lax.broadcasted_iota(jnp.int32, (LANES, WIDE), 0)
    cols = lax.broadcasted_iota(jnp.int32, (LANES, WIDE), 1)
    return jnp.where(cols == 2 * rows + par, 1.0, 0.0).astype(BF)


def uq_kernel(cq_ref, cos_ref, sin_ref, w_hbm, qn_ref, qr_ref, buf, acc, a2, q_scr, h_scr, sems):
    n_chunk = w_hbm.shape[0] // LC
    B = cq_ref.shape[0]
    P = w_hbm.shape[1]
    start_rows(w_hbm, buf.at[0], sems.at[0], 0, LC)
    for par in range(2):
        x = spread(par)
        for k in range(cq_ref.shape[1] // LANES):
            a2[par * B:(par + 1) * B, k * WIDE:(k + 1) * WIDE] = jnp.dot(
                cq_ref[:, k * LANES:(k + 1) * LANES], x, preferred_element_type=F32).astype(BF)
    for c in range(n_chunk):
        slot = c % 2
        if c + 1 < n_chunk:
            start_rows(w_hbm, buf.at[1 - slot], sems.at[1 - slot], (c + 1) * LC, LC)
        pltpu.make_async_copy(buf.at[slot], buf.at[slot], sems.at[slot]).wait()
        lhs = a2[:, c * 2 * LC:(c + 1) * 2 * LC]

        def body(j, _):
            rhs = jnp.concatenate([buf[slot, 2 * j], buf[slot, 2 * j + 1]], axis=1)
            out = jnp.dot(lhs, rhs, preferred_element_type=F32)
            r0 = pl.multiple_of(j * 2 * B, 2 * B)
            if c > 0:
                out = out + acc[pl.ds(r0, 2 * B), :]
            if c < n_chunk - 1:
                acc[pl.ds(r0, 2 * B), :] = out
            else:
                for half in range(2):
                    for par in range(2):
                        q_scr[pl.ds(4 * j + 2 * half + par, B, stride=QS), :] = out[par * B:(par + 1) * B, half * LANES:(half + 1) * LANES]
            return 0
        lax.fori_loop(0, P // 2, body, 0, unroll=8)

    def tb(b, _):
        blk = q_scr[pl.ds(pl.multiple_of(b * QS, 8), 192), :]
        h_scr[pl.ds(b, LANES, stride=HS), :] = blk[:LANES].T
        v = blk[LANES:192].T
        rot = jnp.concatenate([v[:, 32:], v[:, :32]], axis=1)
        qr_ref[b] = (v * cos_ref[pl.ds(b, 1), :] + rot * sin_ref[pl.ds(b, 1), :]).astype(BF)
        return 0
    lax.fori_loop(0, B, tb, 0, unroll=8)

    def hb(h, _):
        qn_ref[h] = h_scr[pl.ds(pl.multiple_of(h * HS, 8), B), :].astype(BF)
        return 0
    lax.fori_loop(0, LANES, hb, 0, unroll=8)


def uq(cq, w_uq, cos2, sin2):
    B, L = cq.shape
    w4 = w_uq.transpose(0, 2, 1).reshape(L, 96, 2, LANES)
    vm = pl.BlockSpec(memory_space=pltpu.VMEM)
    return pl.pallas_call(
        uq_kernel,
        in_specs=[vm, vm, vm, pl.BlockSpec(memory_space=pl.ANY)],
        out_specs=[vm, vm],
        out_shape=[jax.ShapeDtypeStruct((LANES, B, LANES), BF), jax.ShapeDtypeStruct((B, LANES, 64), BF)],
        scratch_shapes=[pltpu.VMEM((2, 96, 2 * LC, LANES), BF), pltpu.VMEM((96 * B, WIDE), F32), pltpu.VMEM((2 * B, 2 * L), BF),
                        pltpu.VMEM((B * QS, LANES), F32), pltpu.VMEM((LANES * HS, LANES), F32), pltpu.SemaphoreType.DMA((2,))],
        compiler_params=pltpu.CompilerParams(vmem_limit_bytes=VMEM_BYTES),
        cost_estimate=pl.CostEstimate(flops=2 * B * L * 24576, bytes_accessed=76 * 10**6, transcendentals=0),
        name="uq",
    )(cq, cos2, sin2, w4)


UL = LANES
KS = 136


def uk_kernel(qn_ref, w_hbm, ql_ref, buf, scr, wd, sel, sems):
    B = qn_ref.shape[1]
    n_chunk = w_hbm.shape[0] // UL
    P = w_hbm.shape[1]
    start_rows(w_hbm, buf.at[0], sems.at[0], 0, UL)
    sel[0:LANES] = spread(0)
    sel[LANES:WIDE] = spread(1)
    for c in range(n_chunk):
        slot = c % 2
        if c + 1 < n_chunk:
            start_rows(w_hbm, buf.at[1 - slot], sems.at[1 - slot], (c + 1) * UL, UL)
        pltpu.make_async_copy(buf.at[slot], buf.at[slot], sems.at[slot]).wait()

        def sort(j, _):
            rhs = jnp.concatenate([buf[slot, 2 * j], buf[slot, 2 * j + 1]], axis=1)
            wd[j] = jnp.dot(sel[...], rhs, preferred_element_type=F32).astype(BF)
            return 0
        lax.fori_loop(0, P // 2, sort, 0, unroll=8)

        def body(j, _):
            for half in range(2):
                for par in range(2):
                    h = 4 * j + 2 * half + par
                    scr[pl.ds(h, B, stride=KS), :] = lax.dot_general(
                        qn_ref[h], wd[j, par * UL:(par + 1) * UL, half * LANES:(half + 1) * LANES],
                        NT, preferred_element_type=F32)
            return 0
        lax.fori_loop(0, P // 2, body, 0, unroll=4)

        def cb(b, _):
            ql_ref[b, :, c * UL:(c + 1) * UL] = scr[pl.ds(pl.multiple_of(b * KS, 8), LANES), :].astype(BF)
            return 0
        lax.fori_loop(0, B, cb, 0, unroll=4)


def uk(qn, w_uk):
    B = qn.shape[1]
    vm = pl.BlockSpec(memory_space=pltpu.VMEM)
    return pl.pallas_call(
        uk_kernel,
        in_specs=[vm, pl.BlockSpec(memory_space=pl.ANY)],
        out_specs=vm,
        out_shape=jax.ShapeDtypeStruct((B, LANES, LATENT), BF),
        scratch_shapes=[pltpu.VMEM((2, 64, 2 * UL, LANES), BF), pltpu.VMEM((B * KS, LANES), F32), pltpu.VMEM((32, WIDE, WIDE), BF), pltpu.VMEM((WIDE, WIDE), BF),
                        pltpu.SemaphoreType.DMA((2,))],
        compiler_params=pltpu.CompilerParams(vmem_limit_bytes=VMEM_BYTES),
        cost_estimate=pl.CostEstimate(flops=2 * B * LANES * LANES * LATENT, bytes_accessed=26 * 10**6, transcendentals=0),
        name="uk",
    )(qn, w_uk.reshape(LATENT, 64, 2, LANES))


NB = 4


def attn_kernel(scale, len_ref, ql_ref, qr_ref, ckv_ref, kpe_ref, cn_ref, kn_ref, ol_ref):
    T = ckv_ref.shape[1]
    dn = NT
    for i in range(NB):
        pos = len_ref[pl.program_id(0) * NB + i]
        row = lax.broadcasted_iota(jnp.int32, ckv_ref.shape[1:], 0)
        ckv = jnp.where(row == pos, cn_ref[i], ckv_ref[i])
        lane = lax.broadcasted_iota(jnp.int32, (LANES, T), 1)
        kn = jnp.broadcast_to(kn_ref[i], (T, 64))
        s_new = lax.dot_general(qr_ref[i], kn, dn, preferred_element_type=F32)
        s_pe = jnp.dot(qr_ref[i], kpe_ref[i], preferred_element_type=F32)
        s = lax.dot_general(ql_ref[i], ckv, dn, preferred_element_type=F32)
        s = (s + jnp.where(lane == pos, s_new, s_pe)) * scale
        s = jnp.where(lane <= pos, s, -jnp.inf)
        e = jnp.exp(s - jnp.max(s, axis=1, keepdims=True))
        den = jnp.sum(e, axis=1, keepdims=True)
        ol = jnp.dot(e.astype(BF), ckv, preferred_element_type=F32)
        ol = (ol / den).astype(BF)
        for k in range(4):
            ol_ref[i, k] = ol[:, k * LANES:(k + 1) * LANES]


def attn(scale, length, ql, qr, ckv, kpe, c_new, k_new):
    B, T, L = ckv.shape
    spec = lambda *s: pl.BlockSpec((NB,) + s, lambda i, _: (i, 0, 0))
    return pl.pallas_call(
        functools.partial(attn_kernel, scale),
        grid_spec=pltpu.PrefetchScalarGridSpec(
            num_scalar_prefetch=1, grid=(B // NB,),
            in_specs=[spec(LANES, L), spec(LANES, 64), spec(T, L), spec(64, T), spec(1, L), spec(1, 64)],
            out_specs=pl.BlockSpec((NB, 4, LANES, LANES), lambda i, _: (i, 0, 0, 0))),
        out_shape=jax.ShapeDtypeStruct((B, 4, LANES, LANES), BF),
        compiler_params=pltpu.CompilerParams(vmem_limit_bytes=40 * 2**20),
        cost_estimate=pl.CostEstimate(flops=2 * B * LANES * T * 1100, bytes_accessed=40 * 10**6, transcendentals=B * LANES * T),
        name="attn",
    )(length, ql, qr, ckv, kpe.transpose(0, 2, 1), c_new.reshape(B, 1, L), k_new.reshape(B, 1, 64))


VP = 16


def uv_kernel(ol_hbm, w_hbm, o_ref, wbuf, abuf, wd, mid, sel, wsems, asem):
    B = ol_hbm.shape[0]
    n_chunk = 64 // VP

    def start_w(c, slot):
        def one(l, _):
            pltpu.make_async_copy(w_hbm.at[l, pl.ds(c * VP, VP)], wbuf.at[slot, :, pl.ds(pl.multiple_of(2 * l, 2), 2), :], wsems.at[slot]).start()
            return 0
        lax.fori_loop(0, LATENT, one, 0, unroll=8)
    def start_a(b, _):
        pltpu.make_async_copy(ol_hbm.at[b], abuf.at[:, :, pl.ds(pl.multiple_of(2 * b, 2), 2), :], asem).start()
        return 0
    lax.fori_loop(0, B, start_a, 0, unroll=8)
    start_w(0, 0)
    sel[0:LANES] = spread(0)
    sel[LANES:WIDE] = spread(1)
    half_rows = lax.broadcasted_iota(jnp.int32, (2 * B, 2 * B), 0)
    half_cols = lax.broadcasted_iota(jnp.int32, (2 * B, 2 * B), 1)
    want = jnp.where(half_rows < B, 2 * half_rows, 2 * (half_rows - B) + 1)
    pick = jnp.where(half_cols == want, 1.0, 0.0).astype(BF)
    pltpu.make_async_copy(abuf, abuf, asem).wait()
    for c in range(n_chunk):
        slot = c % 2
        if c + 1 < n_chunk:
            start_w(c + 1, 1 - slot)
        pltpu.make_async_copy(wbuf.at[slot], wbuf.at[slot], wsems.at[slot]).wait()

        def sort(j, _):
            for k in range(4):
                rows = slice(k * WIDE, (k + 1) * WIDE)
                rhs = jnp.concatenate([wbuf[slot, 2 * j, rows], wbuf[slot, 2 * j + 1, rows]], axis=1)
                w = jnp.dot(sel[...], rhs, preferred_element_type=F32).astype(BF)
                for half in range(2):
                    for par in range(2):
                        wd[2 * j + half, k * LANES:(k + 1) * LANES, par * LANES:(par + 1) * LANES] = w[par * LANES:(par + 1) * LANES, half * LANES:(half + 1) * LANES]
            return 0
        lax.fori_loop(0, VP // 2, sort, 0, unroll=2)

        def body(j, _):
            p = c * VP + j
            lhs = jnp.concatenate([abuf[k, p] for k in range(4)], axis=1)
            mid[j] = jnp.dot(lhs, wd[j], preferred_element_type=F32).astype(BF)
            return 0
        lax.fori_loop(0, VP, body, 0, unroll=4)

        def put(j, _):
            r = jnp.dot(pick, mid[j], preferred_element_type=F32).astype(BF)
            col = pl.multiple_of((c * VP + j) * WIDE, WIDE)
            o_ref[:, pl.ds(col, LANES)] = r[0:B, 0:LANES]
            o_ref[:, pl.ds(col + LANES, LANES)] = r[B:2 * B, LANES:WIDE]
            return 0
        lax.fori_loop(0, VP, put, 0, unroll=4)


def uv(ol, w_uv):
    B = ol.shape[0]
    return pl.pallas_call(
        uv_kernel,
        in_specs=[pl.BlockSpec(memory_space=pl.ANY)] * 2,
        out_specs=pl.BlockSpec(memory_space=pltpu.VMEM),
        out_shape=jax.ShapeDtypeStruct((B, LANES * LANES), BF),
        scratch_shapes=[pltpu.VMEM((2, VP, 1024, LANES), BF), pltpu.VMEM((4, 64, 2 * B, LANES), BF), pltpu.VMEM((VP, LATENT, WIDE), BF), pltpu.VMEM((VP, 2 * B, WIDE), BF), pltpu.VMEM((WIDE, WIDE), BF),
                        pltpu.SemaphoreType.DMA((2,)), pltpu.SemaphoreType.DMA],
        compiler_params=pltpu.CompilerParams(vmem_limit_bytes=VMEM_BYTES),
        cost_estimate=pl.CostEstimate(flops=2 * B * LANES * LANES * LATENT, bytes_accessed=26 * 10**6, transcendentals=0),
        name="uv",
    )(ol.reshape(B, 4, 64, 2, LANES), w_uv.reshape(LATENT, 64, 2, LANES))

def here():
    d = lax.axis_index("dp")
    core = lax.rem(d, 2)
    x = lax.rem(d // 2, 2)
    y = d // 4
    partner = {"dp": d + 1 - 2 * core}
    xn = {"dp": d + 2 - 4 * x}
    yn = {"dp": d + 4 - 8 * y}
    chips = dict(me=2 * y + x, xn=2 * y + 1 - x, yn=2 * (1 - y) + x, diag=2 * (1 - y) + 1 - x)
    return core, chips, partner, xn, yn


def greet(devices):
    barrier = pltpu.get_barrier_semaphore()
    for dev in devices:
        pl.semaphore_signal(barrier, inc=1, device_id=dev, device_id_type=pl.DeviceIdType.MESH)
    pl.semaphore_wait(barrier, len(devices))


def remote(src, dst, send_sem, recv_sem, dev):
    return pltpu.make_async_remote_copy(src_ref=src, dst_ref=dst, send_sem=send_sem, recv_sem=recv_sem,
                                        device_id=dev, device_id_type=pl.DeviceIdType.MESH)


RT = WIDE


def out_kernel(o_ref, x_ref, g_ref, w_hbm, u_ref, r_ref, o2, x2, rall, wbuf, wsems, osems, ssems, rsems):
    core, chips, partner, xn, yn = here()
    me = chips["me"]
    D = x_ref.shape[1]
    half = D // 2
    K = o_ref.shape[1]
    B = o_ref.shape[0]
    n_tile = half // RT
    mine = pl.ds(pl.multiple_of(core * B, B), B)

    def cols(t):
        return pl.ds(pl.multiple_of(core * half + t * RT, RT), RT)

    def load_w(t, slot):
        return pltpu.make_async_copy(w_hbm.at[:, cols(t)], wbuf.at[slot], wsems.at[slot])
    load_w(0, 0).start()
    load_w(1, 1).start()
    greet((partner, xn, yn))
    send_o = remote(o_ref, o2.at[mine], osems.at[0], osems.at[1], partner)
    send_o.start()
    theirs = pl.ds(pl.multiple_of((1 - core) * half, half), half)
    send_x = remote(x_ref.at[:, theirs], x2.at[mine], osems.at[2], osems.at[3], partner)
    send_x.start()
    o2[mine, :] = o_ref[...]
    x2[mine, :] = x_ref[:, pl.ds(pl.multiple_of(core * half, half), half)]

    def copy(flow, t, chip, dev):
        ref = rall.at[chips[chip], :, cols(t)]
        return remote(ref, ref, ssems.at[flow, t], rsems.at[flow, t], dev)

    def arrival(flow, t, chip):
        ref = rall.at[chips[chip], :, cols(t)]
        return remote(ref, ref, ssems.at[flow, t], rsems.at[flow, t], partner)

    def first_forwards(t, par):
        arrival(1, t, "xn").wait_recv()
        copy(3, t, "xn", partner).start()
        if par == 0:
            copy(4, t, "xn", yn).start()
        arrival(2, t, "yn").wait_recv()
        copy(5, t, "yn", partner).start()
        if par == 1:
            copy(4, t, "yn", xn).start()

    def last_forward(t):
        arrival(4, t, "diag").wait_recv()
        copy(6, t, "diag", partner).start()
    send_o.wait()
    send_x.wait()

    def pair(i, _):
        for par in range(2):
            t = 2 * i + par
            load_w(t, par).wait()
            def dot_k(k, acc):
                rows = pl.ds(pl.multiple_of(k * 2048, 2048), 2048)
                return acc + jnp.dot(o2[:, rows], wbuf[par, rows, :], preferred_element_type=F32)
            acc = lax.fori_loop(0, K // 2048, dot_k, jnp.zeros((2 * B, RT), F32), unroll=4)
            xt = x2[:, pl.ds(pl.multiple_of(t * RT, RT), RT)].astype(F32)
            rall[me, :, cols(t)] = (xt + acc).astype(BF)

            @pl.when(i < n_tile // 2 - 1)
            def _():
                load_w(t + 2, par).start()
            copy(0, t, "me", partner).start()
            copy(1, t, "me", xn).start()
            copy(2, t, "me", yn).start()

            @pl.when(i > 0)
            def _():
                first_forwards(t - 2, par)

            @pl.when(i > 1)
            def _():
                last_forward(t - 4)
        return 0
    lax.fori_loop(0, n_tile // 2, pair, 0)
    for par in range(2):
        first_forwards(n_tile - 2 + par, par)
    for t in range(n_tile - 4, n_tile):
        last_forward(t)

    def finish(t, _):
        other = pl.ds(pl.multiple_of((1 - core) * half + t * RT, RT), RT)
        for flow, chip in ((0, "me"), (3, "xn"), (5, "yn"), (6, "diag")):
            ref = rall.at[chips[chip], :, other]
            remote(ref, ref, ssems.at[flow, t], rsems.at[flow, t], partner).wait_recv()
        for flow in range(7):
            arrival(flow, t, "me").wait_send()
        return 0
    lax.fori_loop(0, n_tile, finish, 0)

    def norm(i, _):
        for q in range(4):
            rows = pl.ds(pl.multiple_of(i * 16, 16), 16)
            v = rall[q, rows, :].astype(F32)
            ms = jnp.mean(v * v, axis=1, keepdims=True)
            u_ref[q, rows, :] = (v * lax.rsqrt(ms + EPSILON) * g_ref[...]).astype(BF)
        return 0
    lax.fori_loop(0, 2 * B // 16, norm, 0)
    r_ref[...] = rall[me, mine, :]


def out_proj(o, x, g2, w_out):
    B, D = x.shape
    K = o.shape[1]
    vm = pl.BlockSpec(memory_space=pltpu.VMEM)
    n_tile = D // 2 // RT
    dma = pltpu.SemaphoreType.DMA
    u, r = pl.pallas_call(
        out_kernel,
        in_specs=[vm, vm, vm, pl.BlockSpec(memory_space=pl.ANY)],
        out_specs=[vm, vm],
        out_shape=[jax.ShapeDtypeStruct((4, 2 * B, D), BF), jax.ShapeDtypeStruct((B, D), BF)],
        scratch_shapes=[pltpu.VMEM((2 * B, K), BF), pltpu.VMEM((2 * B, D // 2), BF), pltpu.VMEM((4, 2 * B, D), BF),
                        pltpu.VMEM((2, K, RT), BF), dma((2,)), dma((4,)), dma((7, n_tile)), dma((7, n_tile))],
        compiler_params=pltpu.CompilerParams(vmem_limit_bytes=VMEM_BYTES, collective_id=1, has_side_effects=True),
        cost_estimate=pl.CostEstimate(flops=2 * B * K * D, bytes_accessed=K * D, transcendentals=0),
        name="out_proj",
    )(o, x, g2.reshape(1, D), w_out.reshape(K, D))
    return u.reshape(8 * B, D), r


DT = LATENT


def down_kernel(y_ref, r_ref, w_hbm, out_ref, part, dbuf, ra, rb, wbuf, wsems, ssems, rsems):
    core, chips, partner, xn, yn = here()
    B, D = r_ref.shape
    n_tile = D // DT
    mine = pl.ds(pl.multiple_of(core * B, B), B)
    theirs = pl.ds(pl.multiple_of((1 - core) * B, B), B)

    def load_w(t, slot):
        return pltpu.make_async_copy(w_hbm.at[:, pl.ds(pl.multiple_of(t * DT, DT), DT)], wbuf.at[slot], wsems.at[slot])
    load_w(0, 0).start()
    load_w(1, 1).start()
    greet((partner, xn, yn))

    def swap(t):
        return remote(part.at[t, :, theirs, :], dbuf.at[t], ssems.at[0, t], rsems.at[0, t], partner)

    def first(k, t, par):
        chip = (("xn", "diag"), ("yn", "diag"))[par][k]
        return remote(part.at[t, chips[chip], mine, :], ra.at[t, k], ssems.at[1 + k, t], rsems.at[1 + k, t], (xn, yn)[par])

    def second(t, par):
        return remote(part.at[t, chips[("yn", "xn")[par]], mine, :], rb.at[t], ssems.at[3, t], rsems.at[3, t], (yn, xn)[par])

    def stage_a(t, par):
        swap(t).wait_recv()
        for chip in (("xn", "yn")[par], "diag", ("yn", "xn")[par], "me"):
            q = chips[chip]
            part[t, q, mine, :] = part[t, q, mine, :] + dbuf[t, q]
        for k in (1, 0):
            first(k, t, par).start()

    def pair(i, _):
        for par in range(2):
            t = 2 * i + par
            load_w(t, par).wait()

            def rows(q, _):
                yq = y_ref[pl.ds(pl.multiple_of(q * 2 * B, 2 * B), 2 * B), :]
                part[t, q] = jnp.dot(yq, wbuf[par], preferred_element_type=F32)
                return 0
            lax.fori_loop(0, 4, rows, 0)
            swap(t).start()

            @pl.when(i < n_tile // 2 - 1)
            def _():
                load_w(t + 2, par).start()
            if par == 1:
                stage_a(t - 1, 0)
            else:
                @pl.when(i > 0)
                def _():
                    stage_a(t - 1, 1)
        return 0
    lax.fori_loop(0, n_tile // 2, pair, 0)
    stage_a(n_tile - 1, 1)

    def stage_b(i, _):
        for par in range(2):
            t = 2 * i + par
            first(1, t, par).wait_recv()
            q = chips[("yn", "xn")[par]]
            part[t, q, mine, :] = part[t, q, mine, :] + ra[t, 1]
            second(t, par).start()
        return 0
    lax.fori_loop(0, n_tile // 2, stage_b, 0)

    def stage_c(i, _):
        for par in range(2):
            t = 2 * i + par
            first(0, t, par).wait_recv()
            second(t, par).wait_recv()
            c = pl.ds(pl.multiple_of(t * DT, DT), DT)
            total = part[t, chips["me"], mine, :] + ra[t, 0] + rb[t]
            out_ref[:, c] = (r_ref[:, c].astype(F32) + total).astype(BF)
            swap(t).wait_send()
            first(0, t, par).wait_send()
            first(1, t, par).wait_send()
            second(t, par).wait_send()
        return 0
    lax.fori_loop(0, n_tile // 2, stage_c, 0)


def down(y, r, w_down):
    B, D = r.shape
    K = y.shape[1]
    n_tile = D // DT
    vm = pl.BlockSpec(memory_space=pltpu.VMEM)
    dma = pltpu.SemaphoreType.DMA
    return pl.pallas_call(
        down_kernel,
        in_specs=[vm, vm, pl.BlockSpec(memory_space=pl.ANY)],
        out_specs=vm,
        out_shape=jax.ShapeDtypeStruct((B, D), BF),
        scratch_shapes=[pltpu.VMEM((n_tile, 4, 2 * B, DT), F32), pltpu.VMEM((n_tile, 4, B, DT), F32), pltpu.VMEM((n_tile, 2, B, DT), F32),
                        pltpu.VMEM((n_tile, B, DT), F32), pltpu.VMEM((2, K, DT), BF), dma((2,)), dma((4, n_tile)), dma((4, n_tile))],
        compiler_params=pltpu.CompilerParams(vmem_limit_bytes=VMEM_BYTES, collective_id=2, has_side_effects=True),
        cost_estimate=pl.CostEstimate(flops=2 * 8 * B * K * D, bytes_accessed=2 * K * D, transcendentals=0),
        name="down",
    )(y, r, w_down)


def rms_norm(values_in, gain_vec):
    floats = values_in.astype(jnp.float32)
    mean_sq = jnp.mean(floats * floats, axis=-1, keepdims=True)
    return floats * lax.rsqrt(mean_sq + EPSILON) * gain_vec


def apply_rope(values_in, cos_t, sin_t):
    half_dim = values_in.shape[-1] // 2
    low_half = values_in[..., :half_dim]
    high_half = values_in[..., half_dim:]
    return jnp.concatenate([low_half * cos_t - high_half * sin_t, high_half * cos_t + low_half * sin_t], axis=-1)


def attention_rows(hidden, ckv_cache, kpe_cache, cache_len, rope_cos, rope_sin, norm_attn, w_dq, norm_q, w_uq, w_dkv, norm_kv, w_uk, w_uv):
    value_dim = w_uk.shape[0]
    score_scale = MSCALE * MSCALE / math.sqrt(w_uq.shape[2])
    normed = rms_norm(hidden, norm_attn).astype(BF)
    q_latent = rms_norm(jnp.dot(normed, w_dq, preferred_element_type=jnp.float32), norm_q).astype(BF)
    kv_full = jnp.dot(normed, w_dkv, preferred_element_type=jnp.float32)
    ckv_new = rms_norm(kv_full[:, :value_dim], norm_kv).astype(BF)
    kpe_new = apply_rope(kv_full[:, value_dim:], rope_cos, rope_sin).astype(BF)
    qn, qr = uq(q_latent, w_uq, jnp.concatenate([rope_cos, rope_cos], axis=1), jnp.concatenate([-rope_sin, rope_sin], axis=1))
    ql = uk(qn, w_uk)
    ol = attn(score_scale, cache_len, ql, qr, ckv_cache, kpe_cache, ckv_new, kpe_new)
    head_out = uv(ol, w_uv)
    return head_out, ckv_new, kpe_new


def solution(mesh):
    row_spec = P(('rep', 'dp'), None)
    cube_spec = P(('rep', 'dp'), None, None)
    full_spec = P()
    in_specs = (row_spec, cube_spec, cube_spec, P(('rep', 'dp')), row_spec, row_spec,
                full_spec, full_spec, full_spec, full_spec, full_spec, full_spec, full_spec, full_spec, full_spec, full_spec,
                P(None, 'dp'), P(None, 'dp'), P('dp', None))

    def local_step(hidden, ckv_cache, kpe_cache, cache_len, rope_cos, rope_sin, norm_attn, w_dq, norm_q, w_uq, w_dkv, norm_kv, w_uk, w_uv, w_out, norm_mlp, w_gate, w_up, w_down):
        head_out, ckv_new, kpe_new = attention_rows(hidden, ckv_cache, kpe_cache, cache_len, rope_cos, rope_sin, norm_attn, w_dq, norm_q, w_uq, w_dkv, norm_kv, w_uk, w_uv)
        group_in, residual = out_proj(head_out, hidden, norm_mlp, w_out)
        gate_val = jnp.dot(group_in, w_gate, preferred_element_type=jnp.float32)
        up_val = jnp.dot(group_in, w_up, preferred_element_type=jnp.float32)
        act_val = (jax.nn.silu(gate_val) * up_val).astype(BF)
        out_hidden = down(act_val, residual, w_down)
        return out_hidden, ckv_new, kpe_new

    return jax.shard_map(local_step, mesh=mesh, in_specs=in_specs, out_specs=(row_spec, row_spec, row_spec), check_vma=False)
```

time: 490 us -> 335 us (0.68)
  waiting for transfers between devices: 146 us -> 0 us
  Pallas kernels: 148 us -> 256 us
  matrix products: 166 us -> 63.5 us
  between operations: 14.4 us -> 0.92 us
    pallas_call x0 -> x2, Pallas kernels: none -> 134 us  [the longest x1 73.1 us: down(): pl.pallas_call(down_kernel, in_specs=[vm, vm, pl.BlockSpec(memory_space=p...]
    dot_general x2 -> x0, matrix products: 98.9 us -> none  [the longest x1 72 us: attention_rows(): jnp.dot(head_out, w_out.reshape(-1, w_out.shape[2]), preferred_element_ty...]
    reduce_scatter x1 -> x0, waiting for transfers between devices: 97.1 us -> none  [local_step(): lax.psum_scatter(partial_sum, 'dp', scatter_dimension=0, tiled=True)]
    all_gather x1 -> x0, waiting for transfers between devices: 49 us -> none  [local_step(): group_in = lax.all_gather(mlp_in, 'dp', axis=0, tiled=True)]
    pallas_call x1, Pallas kernels: 43.3 us -> 27.9 us  [uv(): pl.pallas_call(uv_kernel, in_specs=[pl.BlockSpec(memory_space=pl.ANY)] *...]
    pallas_call x1, Pallas kernels: 41.3 us -> 31.8 us  [uk(): pl.pallas_call(uk_kernel, in_specs=[vm, pl.BlockSpec(memory_space=pl.ANY)...]
  transfers between devices with their start and end apart: 2 -> 0, of which waited for: 2 -> 0; matrix products, arithmetic and copies ran while one was open for 0% -> 0% of each run, Pallas kernels for 0% -> 0%
where the time goes in v2:
time: 335 us; the launch traced here: 334 us
  Pallas kernels  256 us (76%)
  matrix products  63.5 us (19%)
  local copies, waits for them, and re-layouts  9.92 us (3%)
  other arithmetic  4.1 us (1%)
    pallas_call x1, Pallas kernels, down(): pl.pallas_call(down_kernel, in_specs=[vm, vm, pl.BlockSpec(memory_space=p...  73.1 us
    pallas_call x1, Pallas kernels, out_proj(): pl.pallas_call(out_kernel, in_specs=[vm, vm, vm, pl.BlockSpec(memory_spac...  61.3 us
    pallas_call x1, Pallas kernels, uq(): pl.pallas_call(uq_kernel, in_specs=[vm, vm, vm, pl.BlockSpec(memory_space...  35.5 us
    pallas_call x1, Pallas kernels, uk(): pl.pallas_call(uk_kernel, in_specs=[vm, pl.BlockSpec(memory_space=pl.ANY)...  31.8 us
    pallas_call x1, Pallas kernels, uv(): pl.pallas_call(uv_kernel, in_specs=[pl.BlockSpec(memory_space=pl.ANY)] *...  27.9 us
    pallas_call x1, Pallas kernels, attn(): pl.pallas_call(functools.partial(attn_kernel, scale), grid_spec=pltpu.Pre...  26.3 us
    dot_general x1, matrix products, local_step(): gate_val = jnp.dot(group_in, w_gate, preferred_element_type=jnp.float32)  24.3 us
    dot_general x1, matrix products, local_step(): up_val = jnp.dot(group_in, w_up, preferred_element_type=jnp.float32)  23.4 us

profile of v2, /device:TPU:0, one launch (start us, length us, event | category | flops | bytes accessed | tf_op | source)
XLA Modules:
  0.0 334.3 jit_solution(9506785438519066438)
XLA Ops:
  0.6 0.0 copy-start.4
  0.6 0.0 copy-start.9
  0.7 0.0 copy-start.5
  0.7 0.0 copy-start.7
  0.7 0.0 copy-start.6
  0.7 1.5 fusion.1
  2.2 0.8 copy.55
  3.0 0.8 copy.58
  3.8 6.2 %fusion.4 = f32[64,576]{1,0:T(8,128)S(1)} fusion(bf16[7168,576]{0,1:T(8,128)(2,1)} %param.29, bf16[64,7168]{1,0:T(8,128)(2,1)} %x_ref.1, f32[7168]{0:T(1024)} %param.25, f32[64]{0:T(128)S(1)} %add_rsqrt_fusion.2), kind=kOutput, calls=%fused_computation.9 | convolution fusion | flops 530317312 | bytes 9351424 | tf_op jit(solution)/shard_map/dot_general | solution.py:540
  10.1 0.1 multiply_reduce_fusion.1
  10.2 0.0 copy-done.9
  10.2 0.1 fusion.16
  10.3 0.7 multiply_convert_fusion.1
  11.0 0.1 fusion.8
  11.1 0.1 copy.66
  11.2 0.1 copy.65
  11.2 0.0 copy-done.7
  11.2 0.0 copy-done.6
  11.3 0.1 copy.57
  11.3 0.7 pad_maximum_fusion
  12.1 0.7 copy.64
  12.8 0.1 copy.62
  12.9 0.1 copy.61
  13.0 0.1 pad_maximum_fusion.2.kn_ref
  13.1 0.1 copy.63.cn_ref
  13.2 0.0 copy-done.4
  13.2 0.0 copy-done.5
  13.2 0.0 copy-start.8
  13.2 9.6 %multiply_reduce_fusion = (f32[64]{0:T(128)S(1)}, f32[64,1536]{1,0:T(8,128)S(1)}) fusion(bf16[7168,1536]{1,0:T(8,128)(2,1)} %param.26, bf16[64,7168]{1,0:T(8,128)(2,1)S(1)} %copy-done.4, f32[7168]{0:T(1024)S(1)} %copy-done.5, f32[64]{0:T(128)S(1)} %add_rsqrt_fusion.2), kind=kOutput, calls=%fused_computation.8 | convolution fusion | flops 1411317760 | bytes 23360000 | tf_op jit(solution)/shard_map/dot_general | solution.py:539
  22.9 0.0 copy-done.8
  22.9 0.8 multiply_convert_fusion.cq_ref
  23.7 35.5 %uq.1 = (bf16[128,64,128]{2,1,0:T(8,128)(2,1)}, bf16[64,128,64]{2,1,0:T(8,128)(2,1)}) custom-call(bf16[64,1536]{1,0:T(8,128)(2,1)} %multiply_convert_fusion.cq_ref, f32[64,64]{1,0:T(8,128)} %get-tuple-element.21.cos_ref, f32[64,64]{1,0:T(8,128)} %get-tuple-element.22.sin_ref, bf16[1536,96,2,128]{3,2,1,0:T(2,128)(2,1)} %bitcast.1.w_hbm), custom_call_target="tpu_custom_call" | custom-call | flops 4831838208 | bytes 76000000 | tf_op jit(solution)/shard_map/uq/pallas_call | solution.py:88
  59.2 0.0 copy-start.1
  59.2 0.0 copy-start.3
  59.2 31.8 %uk.1.ql_ref = bf16[64,128,512]{2,1,0:T(8,128)(2,1)} custom-call(bf16[128,64,128]{2,1,0:T(8,128)(2,1)} %get-tuple-element.7.qn_ref, bf16[512,64,2,128]{3,2,1,0:T(2,128)(2,1)} %bitcast.22), custom_call_target="tpu_custom_call" | custom-call | flops 1073741824 | bytes 26000000 | tf_op jit(solution)/shard_map/uk/pallas_call | solution.py:143
  91.0 0.0 copy-done.1
  91.1 0.0 copy-done.3
  91.1 0.0 copy-start.2
  91.1 1.6 copy-done.2
  92.7 26.3 %attn.1 = bf16[64,4,128,128]{3,2,1,0:T(8,128)(2,1)S(1)} custom-call(s32[64]{0:T(128)S(1)} %copy-done.3, bf16[64,128,512]{2,1,0:T(8,128)(2,1)} %uk.1.ql_ref, bf16[64,128,64]{2,1,0:T(8,128)(2,1)S(1)} %copy-done.2, bf16[64,256,512]{2,1,0:T(8,128)(2,1)} %ckv_ref.1, bf16[64,64,256]{2,1,0:T(8,128)(2,1)S(1)} %bitcast.21, bf16[64,1,512]{2,1,0:T(2,128)(2,1)S(1)} %copy.63.cn_ref, ...), custom_call_target="tpu_custom_call" | custom-call | flops 4613734400 | bytes 40000000 | tf_op jit(solution)/shard_map/attn/pallas_call | solution.py:184
  119.0 0.0 copy-start
  119.0 3.2 copy-done
  122.2 27.9 %uv.1.o_ref = bf16[64,16384]{1,0:T(8,128)(2,1)} custom-call(bf16[64,4,64,2,128]{4,3,2,1,0:T(2,128)(2,1)} %bitcast.20, bf16[512,64,2,128]{3,2,1,0:T(2,128)(2,1)} %bitcast.23), custom_call_target="tpu_custom_call" | custom-call | flops 1073741824 | bytes 26000000 | tf_op jit(solution)/shard_map/uv/pallas_call | solution.py:256
  150.1 61.3 %out_proj.1 = (bf16[4,128,7168]{2,1,0:T(8,128)(2,1)}, bf16[64,7168]{1,0:T(8,128)(2,1)}) custom-call(bf16[64,16384]{1,0:T(8,128)(2,1)} %uv.1.o_ref, bf16[64,7168]{1,0:T(8,128)(2,1)} %x_ref.1, f32[1,7168]{1,0:T(1,128)} %bitcast.26, bf16[16384,7168]{1,0:T(8,128)(2,1)} %bitcast.10.w_hbm), custom_call_target="tpu_custom_call" | custom-call | flops 15032385536 | bytes 117440512 | tf_op jit(solution)/shard_map/out_proj/pallas_call | solution.py:404
  211.4 0.0 copy-start.10
  211.4 24.3 %fusion.9 = f32[512,2304]{1,0:T(8,128)S(1)} fusion(bf16[512,7168]{1,0:T(8,128)(2,1)} %bitcast.27, bf16[7168,2304]{1,0:T(8,128)(2,1)} %param.35), kind=kOutput, calls=%fused_computation.23 | convolution fusion | flops 16911433728 | bytes 45088768 | tf_op jit(solution)/shard_map/dot_general | solution.py:561
  235.7 0.0 copy-done.10
  235.7 23.4 %fusion.y_ref = bf16[512,2304]{1,0:T(8,128)(2,1)} fusion(bf16[512,7168]{1,0:T(8,128)(2,1)S(1)} %bitcast.28, bf16[7168,2304]{1,0:T(8,128)(2,1)} %param.36, f32[512,2304]{1,0:T(8,128)S(1)} %fusion.9), kind=kOutput, calls=%fused_computation.1 | convolution fusion | flops 16918511616 | bytes 47448064 | tf_op jit(solution)/shard_map/dot_general | solution.py:562
  259.0 73.1 %down.1 = bf16[64,7168]{1,0:T(8,128)(2,1)} custom-call(bf16[512,2304]{1,0:T(8,128)(2,1)} %fusion.y_ref, bf16[64,7168]{1,0:T(8,128)(2,1)} %get-tuple-element.10.r_ref, bf16[2304,7168]{1,0:T(8,128)(2,1)} %w_hbm.1), custom_call_target="tpu_custom_call" | custom-call | flops 16911433728 | bytes 33030144 | tf_op jit(solution)/shard_map/down/pallas_call | solution.py:509
  332.1 2.2 copy.68
  (5 shorter events, 0.0 us)
Async XLA Ops:
  0.6 12.6 %copy-start.4 = (bf16[64,7168]{1,0:T(8,128)(2,1)S(1)}, bf16[64,7168]{1,0:T(8,128)(2,1)}, u32[]{:S(2)}) copy-start(bf16[64,7168]{1,0:T(8,128)(2,1)} %x_ref.1) | copy-start | bytes 2752516
  0.6 9.6 %copy-start.9 = (f32[512]{0:T(512)S(1)}, f32[512]{0:T(512)}, u32[]{:S(2)}) copy-start(f32[512]{0:T(512)} %param.30) | copy-start | bytes 6148
  0.7 12.6 %copy-start.5 = (f32[7168]{0:T(1024)S(1)}, f32[7168]{0:T(1024)}, u32[]{:S(2)}) copy-start(f32[7168]{0:T(1024)} %param.25) | copy-start | bytes 86020
  0.7 10.6 %copy-start.7 = (f32[64,32]{0,1:T(8,128)S(1)}, f32[64,32]{0,1:T(8,128)}, u32[]{:S(2)}) copy-start(f32[64,32]{0,1:T(8,128)} %param.24) | copy-start | bytes 24580
  0.7 10.6 %copy-start.6 = (f32[64,32]{0,1:T(8,128)S(1)}, f32[64,32]{0,1:T(8,128)}, u32[]{:S(2)}) copy-start(f32[64,32]{0,1:T(8,128)} %param.23) | copy-start | bytes 24580
  13.2 9.7 %copy-start.8 = (f32[1536]{0:T(1024)S(1)}, f32[1536]{0:T(1024)}, u32[]{:S(2)}) copy-start(f32[1536]{0:T(1024)} %param.27) | copy-start | bytes 18436
  59.2 31.9 %copy-start.1 = (bf16[64,256,64]{1,2,0:T(8,128)(2,1)S(1)}, bf16[64,256,64]{1,2,0:T(8,128)(2,1)}, u32[]{:S(2)}) copy-start(bf16[64,256,64]{1,2,0:T(8,128)(2,1)} %param.21) | copy-start | bytes 6291460
  59.2 31.9 %copy-start.3 = (s32[64]{0:T(128)S(1)}, s32[64]{0:T(128)}, u32[]{:S(2)}) copy-start(s32[64]{0:T(128)} %len_ref.1) | copy-start | bytes 772
  91.1 1.6 copy-start.2
  119.0 3.2 copy-start
  211.4 24.3 %copy-start.10 = (bf16[4,128,7168]{2,1,0:T(8,128)(2,1)S(1)}, bf16[4,128,7168]{2,1,0:T(8,128)(2,1)}, u32[]{:S(2)}) copy-start(bf16[4,128,7168]{2,1,0:T(8,128)(2,1)} %get-tuple-element.9) | copy-start | bytes 22020100

commit v3 on v2

--- a/solution.py
+++ b/solution.py
@@ -21,11 +21,15 @@
 LC = 256
 
 
+def loop(count, body, unroll=1):
+    lax.fori_loop(0, count, body, 0, unroll=unroll)
+
+
 def start_rows(w_hbm, buf, sem, l0, count):
     def one(l, _):
         pltpu.make_async_copy(w_hbm.at[l0 + l], buf.at[:, pl.ds(pl.multiple_of(2 * l, 2), 2), :], sem).start()
         return 0
-    lax.fori_loop(0, count, one, 0, unroll=8)
+    loop(count, one, unroll=8)
 
 
 def spread(par):
@@ -64,7 +68,7 @@
                     for par in range(2):
                         q_scr[pl.ds(4 * j + 2 * half + par, B, stride=QS), :] = out[par * B:(par + 1) * B, half * LANES:(half + 1) * LANES]
             return 0
-        lax.fori_loop(0, P // 2, body, 0, unroll=8)
+        loop(P // 2, body, unroll=8)
 
     def tb(b, _):
         blk = q_scr[pl.ds(pl.multiple_of(b * QS, 8), 192), :]
@@ -73,12 +77,12 @@
         rot = jnp.concatenate([v[:, 32:], v[:, :32]], axis=1)
         qr_ref[b] = (v * cos_ref[pl.ds(b, 1), :] + rot * sin_ref[pl.ds(b, 1), :]).astype(BF)
         return 0
-    lax.fori_loop(0, B, tb, 0, unroll=8)
+    loop(B, tb, unroll=8)
 
     def hb(h, _):
         qn_ref[h] = h_scr[pl.ds(pl.multiple_of(h * HS, 8), B), :].astype(BF)
         return 0
-    lax.fori_loop(0, LANES, hb, 0, unroll=8)
+    loop(LANES, hb, unroll=8)
 
 
 def uq(cq, w_uq, cos2, sin2):
@@ -119,7 +123,7 @@
             rhs = jnp.concatenate([buf[slot, 2 * j], buf[slot, 2 * j + 1]], axis=1)
             wd[j] = jnp.dot(sel[...], rhs, preferred_element_type=F32).astype(BF)
             return 0
-        lax.fori_loop(0, P // 2, sort, 0, unroll=8)
+        loop(P // 2, sort, unroll=8)
 
         def body(j, _):
             for half in range(2):
@@ -129,12 +133,12 @@
                         qn_ref[h], wd[j, par * UL:(par + 1) * UL, half * LANES:(half + 1) * LANES],
                         NT, preferred_element_type=F32)
             return 0
-        lax.fori_loop(0, P // 2, body, 0, unroll=4)
+        loop(P // 2, body, unroll=4)
 
         def cb(b, _):
             ql_ref[b, :, c * UL:(c + 1) * UL] = scr[pl.ds(pl.multiple_of(b * KS, 8), LANES), :].astype(BF)
             return 0
-        lax.fori_loop(0, B, cb, 0, unroll=4)
+        loop(B, cb, unroll=4)
 
 
 def uk(qn, w_uk):
@@ -205,11 +209,11 @@
         def one(l, _):
             pltpu.make_async_copy(w_hbm.at[l, pl.ds(c * VP, VP)], wbuf.at[slot, :, pl.ds(pl.multiple_of(2 * l, 2), 2), :], wsems.at[slot]).start()
             return 0
-        lax.fori_loop(0, LATENT, one, 0, unroll=8)
+        loop(LATENT, one, unroll=8)
     def start_a(b, _):
         pltpu.make_async_copy(ol_hbm.at[b], abuf.at[:, :, pl.ds(pl.multiple_of(2 * b, 2), 2), :], asem).start()
         return 0
-    lax.fori_loop(0, B, start_a, 0, unroll=8)
+    loop(B, start_a, unroll=8)
     start_w(0, 0)
     sel[0:LANES] = spread(0)
     sel[LANES:WIDE] = spread(1)
@@ -233,14 +237,14 @@
                     for par in range(2):
                         wd[2 * j + half, k * LANES:(k + 1) * LANES, par * LANES:(par + 1) * LANES] = w[par * LANES:(par + 1) * LANES, half * LANES:(half + 1) * LANES]
             return 0
-        lax.fori_loop(0, VP // 2, sort, 0, unroll=2)
+        loop(VP // 2, sort, unroll=2)
 
         def body(j, _):
             p = c * VP + j
             lhs = jnp.concatenate([abuf[k, p] for k in range(4)], axis=1)
             mid[j] = jnp.dot(lhs, wd[j], preferred_element_type=F32).astype(BF)
             return 0
-        lax.fori_loop(0, VP, body, 0, unroll=4)
+        loop(VP, body, unroll=4)
 
         def put(j, _):
             r = jnp.dot(pick, mid[j], preferred_element_type=F32).astype(BF)
@@ -248,7 +252,7 @@
             o_ref[:, pl.ds(col, LANES)] = r[0:B, 0:LANES]
             o_ref[:, pl.ds(col + LANES, LANES)] = r[B:2 * B, LANES:WIDE]
             return 0
-        lax.fori_loop(0, VP, put, 0, unroll=4)
+        loop(VP, put, unroll=4)
 
 
 def uv(ol, w_uv):
@@ -368,7 +372,7 @@
             def _():
                 last_forward(t - 4)
         return 0
-    lax.fori_loop(0, n_tile // 2, pair, 0)
+    loop(n_tile // 2, pair)
     for par in range(2):
         first_forwards(n_tile - 2 + par, par)
     for t in range(n_tile - 4, n_tile):
@@ -382,16 +386,16 @@
         for flow in range(7):
             arrival(flow, t, "me").wait_send()
         return 0
-    lax.fori_loop(0, n_tile, finish, 0)
+    loop(n_tile, finish)
 
     def norm(i, _):
-        for q in range(4):
+        for k, chip in enumerate(("me", "xn", "yn", "diag")):
             rows = pl.ds(pl.multiple_of(i * 16, 16), 16)
-            v = rall[q, rows, :].astype(F32)
+            v = rall[chips[chip], rows, :].astype(F32)
             ms = jnp.mean(v * v, axis=1, keepdims=True)
-            u_ref[q, rows, :] = (v * lax.rsqrt(ms + EPSILON) * g_ref[...]).astype(BF)
-        return 0
-    lax.fori_loop(0, 2 * B // 16, norm, 0)
+            u_ref[k, rows, :] = (v * lax.rsqrt(ms + EPSILON) * g_ref[...]).astype(BF)
+        return 0
+    loop(2 * B // 16, norm)
     r_ref[...] = rall[me, mine, :]
 
 
@@ -416,107 +420,149 @@
 
 
 DT = LATENT
-
-
-def down_kernel(y_ref, r_ref, w_hbm, out_ref, part, dbuf, ra, rb, wbuf, wsems, ssems, rsems):
+GT = LANES
+
+
+def mlp_kernel(u_ref, r_ref, wg_hbm, wu_hbm, w_hbm, out_ref, y, part, dbuf, ra, rb, gbuf, ubuf, wbuf, gsems, usems, wsems, ssems, rsems):
     core, chips, partner, xn, yn = here()
     B, D = r_ref.shape
-    n_tile = D // DT
-    mine = pl.ds(pl.multiple_of(core * B, B), B)
-    theirs = pl.ds(pl.multiple_of((1 - core) * B, B), B)
+    n_gate, n_tile = wg_hbm.shape[1] // GT, D // DT
+    near, side, far = (1, 2), (2, 1), 3
+    others, own = slice(2 * B, 8 * B), slice(0, 2 * B)
+
+    def load_g(n, slot):
+        c = pl.ds(pl.multiple_of(n * GT, GT), GT)
+        return (pltpu.make_async_copy(wg_hbm.at[:, c], gbuf.at[slot], gsems.at[slot]),
+                pltpu.make_async_copy(wu_hbm.at[:, c], ubuf.at[slot], usems.at[slot]))
 
     def load_w(t, slot):
         return pltpu.make_async_copy(w_hbm.at[:, pl.ds(pl.multiple_of(t * DT, DT), DT)], wbuf.at[slot], wsems.at[slot])
-    load_w(0, 0).start()
-    load_w(1, 1).start()
+
+    for slot in range(2):
+        for cp in load_g(slot, slot):
+            cp.start()
+    for slot in range(2):
+        load_w(slot, slot).start()
     greet((partner, xn, yn))
 
-    def swap(t):
-        return remote(part.at[t, :, theirs, :], dbuf.at[t], ssems.at[0, t], rsems.at[0, t], partner)
+    def gate_up(which, more):
+        def step(n, _):
+            slot = lax.rem(n, 2)
+            for cp in load_g(n, slot):
+                cp.wait()
+
+            uq = u_ref[which, :]
+            both = jnp.dot(uq, jnp.concatenate([gbuf[slot], ubuf[slot]], axis=1), preferred_element_type=F32)
+            y[which, pl.ds(pl.multiple_of(n * GT, GT), GT)] = (jax.nn.silu(both[:, :GT]) * both[:, GT:]).astype(BF)
+
+            @pl.when(n < n_gate - 2)
+            def _():
+                for cp in load_g(n + 2, slot):
+                    cp.start()
+            if more:
+                @pl.when(n >= n_gate - 2)
+                def _():
+                    for cp in load_g(slot, slot):
+                        cp.start()
+            return 0
+        loop(n_gate, step)
+
+    def mine(k):
+        return pl.ds(pl.multiple_of((2 * k + core) * B, B), B)
+
+    def theirs(k):
+        return pl.ds(pl.multiple_of((2 * k + 1 - core) * B, B), B)
+
+    def swap(k, t):
+        return remote(part.at[t, theirs(k), :], dbuf.at[t, k], ssems.at[3 + k, t], rsems.at[3 + k, t], partner)
 
     def first(k, t, par):
-        chip = (("xn", "diag"), ("yn", "diag"))[par][k]
-        return remote(part.at[t, chips[chip], mine, :], ra.at[t, k], ssems.at[1 + k, t], rsems.at[1 + k, t], (xn, yn)[par])
+        return remote(part.at[t, mine((near[par], far)[k]), :], ra.at[t, k], ssems.at[k, t], rsems.at[k, t], (xn, yn)[par])
 
     def second(t, par):
-        return remote(part.at[t, chips[("yn", "xn")[par]], mine, :], rb.at[t], ssems.at[3, t], rsems.at[3, t], (yn, xn)[par])
+        return remote(part.at[t, mine(side[par]), :], rb.at[t], ssems.at[2, t], rsems.at[2, t], (yn, xn)[par])
 
     def stage_a(t, par):
-        swap(t).wait_recv()
-        for chip in (("xn", "yn")[par], "diag", ("yn", "xn")[par], "me"):
-            q = chips[chip]
-            part[t, q, mine, :] = part[t, q, mine, :] + dbuf[t, q]
+        for k in (far, near[par], side[par]):
+            swap(k, t).wait_recv()
+            part[t, mine(k), :] = part[t, mine(k), :] + dbuf[t, k]
         for k in (1, 0):
             first(k, t, par).start()
 
-    def pair(i, _):
-        for par in range(2):
-            t = 2 * i + par
-            load_w(t, par).wait()
-
-            def rows(q, _):
-                yq = y_ref[pl.ds(pl.multiple_of(q * 2 * B, 2 * B), 2 * B), :]
-                part[t, q] = jnp.dot(yq, wbuf[par], preferred_element_type=F32)
-                return 0
-            lax.fori_loop(0, 4, rows, 0)
-            swap(t).start()
-
-            @pl.when(i < n_tile // 2 - 1)
-            def _():
-                load_w(t + 2, par).start()
-            if par == 1:
-                stage_a(t - 1, 0)
-            else:
-                @pl.when(i > 0)
+    def down(which, send, more, after):
+        def pair(i, _):
+            for par in range(2):
+                t = 2 * i + par
+                load_w(t, par).wait()
+
+                part[t, which, :] = jnp.dot(y[which, :], wbuf[par], preferred_element_type=F32)
+                for k in send:
+                    swap(k, t).start()
+
+                @pl.when(i < n_tile // 2 - 1)
                 def _():
-                    stage_a(t - 1, 1)
-        return 0
-    lax.fori_loop(0, n_tile // 2, pair, 0)
+                    load_w(t + 2, par).start()
+                if more:
+                    @pl.when(i == n_tile // 2 - 1)
+                    def _():
+                        load_w(par, par).start()
+                if after and par == 1:
+                    after(t - 1, 0)
+                elif after:
+                    @pl.when(i > 0)
+                    def _():
+                        after(t - 1, 1)
+            return 0
+        loop(n_tile // 2, pair)
+
+    gate_up(others, True)
+    down(others, (3, 1, 2), True, stage_a)
     stage_a(n_tile - 1, 1)
+    gate_up(own, False)
+    down(own, (0,), False, None)
 
     def stage_b(i, _):
         for par in range(2):
             t = 2 * i + par
             first(1, t, par).wait_recv()
-            q = chips[("yn", "xn")[par]]
-            part[t, q, mine, :] = part[t, q, mine, :] + ra[t, 1]
+            part[t, mine(side[par]), :] = part[t, mine(side[par]), :] + ra[t, 1]
             second(t, par).start()
         return 0
-    lax.fori_loop(0, n_tile // 2, stage_b, 0)
+    loop(n_tile // 2, stage_b)
 
     def stage_c(i, _):
         for par in range(2):
             t = 2 * i + par
+            swap(0, t).wait_recv()
             first(0, t, par).wait_recv()
             second(t, par).wait_recv()
             c = pl.ds(pl.multiple_of(t * DT, DT), DT)
-            total = part[t, chips["me"], mine, :] + ra[t, 0] + rb[t]
+            total = part[t, mine(0), :] + dbuf[t, 0] + ra[t, 0] + rb[t]
             out_ref[:, c] = (r_ref[:, c].astype(F32) + total).astype(BF)
-            swap(t).wait_send()
-            first(0, t, par).wait_send()
-            first(1, t, par).wait_send()
-            second(t, par).wait_send()
-        return 0
-    lax.fori_loop(0, n_tile // 2, stage_c, 0)
-
-
-def down(y, r, w_down):
+            for cp in (swap(0, t), swap(1, t), swap(2, t), swap(3, t), first(0, t, par), first(1, t, par), second(t, par)):
+                cp.wait_send()
+        return 0
+    loop(n_tile // 2, stage_c)
+
+
+def mlp(u, r, w_gate, w_up, w_down):
     B, D = r.shape
-    K = y.shape[1]
+    K = w_down.shape[0]
     n_tile = D // DT
     vm = pl.BlockSpec(memory_space=pltpu.VMEM)
     dma = pltpu.SemaphoreType.DMA
     return pl.pallas_call(
-        down_kernel,
-        in_specs=[vm, vm, pl.BlockSpec(memory_space=pl.ANY)],
+        mlp_kernel,
+        in_specs=[vm, vm] + [pl.BlockSpec(memory_space=pl.ANY)] * 3,
         out_specs=vm,
         out_shape=jax.ShapeDtypeStruct((B, D), BF),
-        scratch_shapes=[pltpu.VMEM((n_tile, 4, 2 * B, DT), F32), pltpu.VMEM((n_tile, 4, B, DT), F32), pltpu.VMEM((n_tile, 2, B, DT), F32),
-                        pltpu.VMEM((n_tile, B, DT), F32), pltpu.VMEM((2, K, DT), BF), dma((2,)), dma((4, n_tile)), dma((4, n_tile))],
+        scratch_shapes=[pltpu.VMEM((8 * B, K), BF), pltpu.VMEM((n_tile, 8 * B, DT), F32), pltpu.VMEM((n_tile, 4, B, DT), F32),
+                        pltpu.VMEM((n_tile, 2, B, DT), F32), pltpu.VMEM((n_tile, B, DT), F32), pltpu.VMEM((2, D, GT), BF),
+                        pltpu.VMEM((2, D, GT), BF), pltpu.VMEM((2, K, DT), BF), dma((2,)), dma((2,)), dma((2,)), dma((7, n_tile)), dma((7, n_tile))],
         compiler_params=pltpu.CompilerParams(vmem_limit_bytes=VMEM_BYTES, collective_id=2, has_side_effects=True),
-        cost_estimate=pl.CostEstimate(flops=2 * 8 * B * K * D, bytes_accessed=2 * K * D, transcendentals=0),
-        name="down",
-    )(y, r, w_down)
+        cost_estimate=pl.CostEstimate(flops=48 * B * K * D, bytes_accessed=6 * K * D, transcendentals=0),
+        name="mlp",
+    )(u, r, w_gate, w_up, w_down)
 
 
 def rms_norm(values_in, gain_vec):
@@ -558,10 +604,7 @@
     def local_step(hidden, ckv_cache, kpe_cache, cache_len, rope_cos, rope_sin, norm_attn, w_dq, norm_q, w_uq, w_dkv, norm_kv, w_uk, w_uv, w_out, norm_mlp, w_gate, w_up, w_down):
         head_out, ckv_new, kpe_new = attention_rows(hidden, ckv_cache, kpe_cache, cache_len, rope_cos, rope_sin, norm_attn, w_dq, norm_q, w_uq, w_dkv, norm_kv, w_uk, w_uv)
         group_in, residual = out_proj(head_out, hidden, norm_mlp, w_out)
-        gate_val = jnp.dot(group_in, w_gate, preferred_element_type=jnp.float32)
-        up_val = jnp.dot(group_in, w_up, preferred_element_type=jnp.float32)
-        act_val = (jax.nn.silu(gate_val) * up_val).astype(BF)
-        out_hidden = down(act_val, residual, w_down)
+        out_hidden = mlp(group_in, residual, w_gate, w_up, w_down)
         return out_hidden, ckv_new, kpe_new
 
     return jax.shard_map(local_step, mesh=mesh, in_specs=in_specs, out_specs=(row_spec, row_spec, row_spec), check_vma=False)

time: 335 us -> 336 us (level)
  Pallas kernels: 256 us -> 304 us
  matrix products: 63.5 us -> 15.9 us
    pallas_call x1, Pallas kernels: 73.1 us -> 122 us  [mlp(): pl.pallas_call(mlp_kernel, in_specs=[vm, vm] + [pl.BlockSpec(memory_space...]
    dot_general x2 -> x0, matrix products: 47.6 us -> none  [the longest x1 24.3 us: local_step(): gate_val = jnp.dot(group_in, w_gate, preferred_element_type=jnp.float32)]
    unnamed x28 -> x26, local copies, waits for them, and re-layouts: 9.47 us -> 9.47 us
where the time goes in v3:
time: 336 us; the launch traced here: 335 us
  Pallas kernels  304 us (90%)
  matrix products  15.9 us (5%)
  local copies, waits for them, and re-layouts  9.92 us (3%)
  other arithmetic  4.08 us (1%)
    pallas_call x1, Pallas kernels, mlp(): pl.pallas_call(mlp_kernel, in_specs=[vm, vm] + [pl.BlockSpec(memory_space...  122 us
    pallas_call x1, Pallas kernels, out_proj(): pl.pallas_call(out_kernel, in_specs=[vm, vm, vm, pl.BlockSpec(memory_spac...  61.3 us
    pallas_call x1, Pallas kernels, uq(): pl.pallas_call(uq_kernel, in_specs=[vm, vm, vm, pl.BlockSpec(memory_space...  35.4 us
    pallas_call x1, Pallas kernels, uk(): pl.pallas_call(uk_kernel, in_specs=[vm, pl.BlockSpec(memory_space=pl.ANY)...  31.7 us
    pallas_call x1, Pallas kernels, uv(): pl.pallas_call(uv_kernel, in_specs=[pl.BlockSpec(memory_space=pl.ANY)] *...  27.8 us
    pallas_call x1, Pallas kernels, attn(): pl.pallas_call(functools.partial(attn_kernel, scale), grid_spec=pltpu.Pre...  26.3 us
    dot_general x1, matrix products, attention_rows(): jnp.dot(normed, w_dq, preferred_element_type=jnp.float32)  9.64 us
    unnamed x26, local copies, waits for them, and re-layouts  9.47 us

profile of v3, /device:TPU:0, one launch (start us, length us, event | category | flops | bytes accessed | tf_op | source)
XLA Modules:
  0.0 334.8 jit_solution(3597772985281616281)
XLA Ops:
  0.6 0.0 copy-start.4
  0.6 0.0 copy-start.9
  0.7 0.0 copy-start.5
  0.7 0.0 copy-start.7
  0.7 0.0 copy-start.6
  0.7 1.5 fusion
  2.2 0.8 copy.55
  3.0 0.8 copy.58
  3.8 6.2 %fusion.3 = f32[64,576]{1,0:T(8,128)S(1)} fusion(bf16[7168,576]{0,1:T(8,128)(2,1)} %param.29, bf16[64,7168]{1,0:T(8,128)(2,1)} %x_ref.1, f32[7168]{0:T(1024)} %param.25, f32[64]{0:T(128)S(1)} %add_rsqrt_fusion.2), kind=kOutput, calls=%fused_computation.7 | convolution fusion | flops 530317312 | bytes 9351424 | tf_op jit(solution)/shard_map/dot_general | solution.py:586
  10.1 0.1 multiply_reduce_fusion.1
  10.2 0.0 copy-done.9
  10.2 0.1 fusion.10
  10.3 0.7 multiply_convert_fusion.1
  11.0 0.1 fusion.7
  11.1 0.1 copy.66
  11.2 0.1 copy.65
  11.2 0.0 copy-done.7
  11.2 0.0 copy-done.6
  11.3 0.1 copy.57
  11.3 0.7 pad_maximum_fusion
  12.1 0.7 copy.64
  12.8 0.1 copy.62
  12.9 0.1 copy.61
  13.0 0.1 pad_maximum_fusion.2.kn_ref
  13.1 0.1 copy.63.cn_ref
  13.2 0.0 copy-done.4
  13.2 0.0 copy-done.5
  13.2 0.0 copy-start.8
  13.2 9.6 %multiply_reduce_fusion = (f32[64]{0:T(128)S(1)}, f32[64,1536]{1,0:T(8,128)S(1)}) fusion(bf16[7168,1536]{1,0:T(8,128)(2,1)} %param.26, bf16[64,7168]{1,0:T(8,128)(2,1)S(1)} %copy-done.4, f32[7168]{0:T(1024)S(1)} %copy-done.5, f32[64]{0:T(128)S(1)} %add_rsqrt_fusion.2), kind=kOutput, calls=%fused_computation.6 | convolution fusion | flops 1411317760 | bytes 23360000 | tf_op jit(solution)/shard_map/dot_general | solution.py:585
  22.9 0.0 copy-done.8
  22.9 0.8 multiply_convert_fusion.cq_ref
  23.7 35.4 %uq.1 = (bf16[128,64,128]{2,1,0:T(8,128)(2,1)}, bf16[64,128,64]{2,1,0:T(8,128)(2,1)}) custom-call(bf16[64,1536]{1,0:T(8,128)(2,1)} %multiply_convert_fusion.cq_ref, f32[64,64]{1,0:T(8,128)} %get-tuple-element.21.cos_ref, f32[64,64]{1,0:T(8,128)} %get-tuple-element.22.sin_ref, bf16[1536,96,2,128]{3,2,1,0:T(2,128)(2,1)} %bitcast.1.w_hbm), custom_call_target="tpu_custom_call" | custom-call | flops 4831838208 | bytes 76000000 | tf_op jit(solution)/shard_map/uq/pallas_call | solution.py:92
  59.1 0.0 copy-start.1
  59.1 0.0 copy-start.3
  59.1 31.7 %uk.1.ql_ref = bf16[64,128,512]{2,1,0:T(8,128)(2,1)} custom-call(bf16[128,64,128]{2,1,0:T(8,128)(2,1)} %get-tuple-element.7.qn_ref, bf16[512,64,2,128]{3,2,1,0:T(2,128)(2,1)} %bitcast.18), custom_call_target="tpu_custom_call" | custom-call | flops 1073741824 | bytes 26000000 | tf_op jit(solution)/shard_map/uk/pallas_call | solution.py:147
  90.8 0.0 copy-done.1
  90.8 0.0 copy-done.3
  90.8 0.0 copy-start.2
  90.9 1.6 copy-done.2
  92.4 26.3 %attn.1 = bf16[64,4,128,128]{3,2,1,0:T(8,128)(2,1)S(1)} custom-call(s32[64]{0:T(128)S(1)} %copy-done.3, bf16[64,128,512]{2,1,0:T(8,128)(2,1)} %uk.1.ql_ref, bf16[64,128,64]{2,1,0:T(8,128)(2,1)S(1)} %copy-done.2, bf16[64,256,512]{2,1,0:T(8,128)(2,1)} %ckv_ref.1, bf16[64,64,256]{2,1,0:T(8,128)(2,1)S(1)} %bitcast.17, bf16[64,1,512]{2,1,0:T(2,128)(2,1)S(1)} %copy.63.cn_ref, ...), custom_call_target="tpu_custom_call" | custom-call | flops 4613734400 | bytes 40000000 | tf_op jit(solution)/shard_map/attn/pallas_call | solution.py:188
  118.8 0.0 copy-start
  118.8 3.2 copy-done
  122.0 27.8 %uv.1.o_ref = bf16[64,16384]{1,0:T(8,128)(2,1)} custom-call(bf16[64,4,64,2,128]{4,3,2,1,0:T(2,128)(2,1)} %bitcast.16, bf16[512,64,2,128]{3,2,1,0:T(2,128)(2,1)} %bitcast.19), custom_call_target="tpu_custom_call" | custom-call | flops 1073741824 | bytes 26000000 | tf_op jit(solution)/shard_map/uv/pallas_call | solution.py:260
  149.8 61.3 %out_proj.1 = (bf16[4,128,7168]{2,1,0:T(8,128)(2,1)}, bf16[64,7168]{1,0:T(8,128)(2,1)}) custom-call(bf16[64,16384]{1,0:T(8,128)(2,1)} %uv.1.o_ref, bf16[64,7168]{1,0:T(8,128)(2,1)} %x_ref.1, f32[1,7168]{1,0:T(1,128)} %bitcast.22, bf16[16384,7168]{1,0:T(8,128)(2,1)} %bitcast.10.w_hbm), custom_call_target="tpu_custom_call" | custom-call | flops 15032385536 | bytes 117440512 | tf_op jit(solution)/shard_map/out_proj/pallas_call | solution.py:408
  211.1 121.5 %mlp.1 = bf16[64,7168]{1,0:T(8,128)(2,1)} custom-call(bf16[512,7168]{1,0:T(8,128)(2,1)} %bitcast.23, bf16[64,7168]{1,0:T(8,128)(2,1)} %get-tuple-element.10.r_ref, bf16[7168,2304]{1,0:T(8,128)(2,1)} %wg_hbm.1, bf16[7168,2304]{1,0:T(8,128)(2,1)} %wu_hbm.1, bf16[2304,7168]{1,0:T(8,128)(2,1)} %w_hbm.1), custom_call_target="tpu_custom_call" | custom-call | flops 50734301184 | bytes 99090432 | tf_op jit(solution)/shard_map/mlp/pallas_call | solution.py:554
  332.7 2.2 copy.68
  (5 shorter events, 0.0 us)
Async XLA Ops:
  0.6 12.6 %copy-start.4 = (bf16[64,7168]{1,0:T(8,128)(2,1)S(1)}, bf16[64,7168]{1,0:T(8,128)(2,1)}, u32[]{:S(2)}) copy-start(bf16[64,7168]{1,0:T(8,128)(2,1)} %x_ref.1) | copy-start | bytes 2752516
  0.6 9.6 %copy-start.9 = (f32[512]{0:T(512)S(1)}, f32[512]{0:T(512)}, u32[]{:S(2)}) copy-start(f32[512]{0:T(512)} %param.30) | copy-start | bytes 6148
  0.7 12.6 %copy-start.5 = (f32[7168]{0:T(1024)S(1)}, f32[7168]{0:T(1024)}, u32[]{:S(2)}) copy-start(f32[7168]{0:T(1024)} %param.25) | copy-start | bytes 86020
  0.7 10.6 %copy-start.7 = (f32[64,32]{0,1:T(8,128)S(1)}, f32[64,32]{0,1:T(8,128)}, u32[]{:S(2)}) copy-start(f32[64,32]{0,1:T(8,128)} %param.24) | copy-start | bytes 24580
  0.7 10.6 %copy-start.6 = (f32[64,32]{0,1:T(8,128)S(1)}, f32[64,32]{0,1:T(8,128)}, u32[]{:S(2)}) copy-start(f32[64,32]{0,1:T(8,128)} %param.23) | copy-start | bytes 24580
  13.2 9.7 %copy-start.8 = (f32[1536]{0:T(1024)S(1)}, f32[1536]{0:T(1024)}, u32[]{:S(2)}) copy-start(f32[1536]{0:T(1024)} %param.27) | copy-start | bytes 18436
  59.1 31.8 %copy-start.1 = (bf16[64,256,64]{1,2,0:T(8,128)(2,1)S(1)}, bf16[64,256,64]{1,2,0:T(8,128)(2,1)}, u32[]{:S(2)}) copy-start(bf16[64,256,64]{1,2,0:T(8,128)(2,1)} %param.21) | copy-start | bytes 6291460
  59.1 31.8 %copy-start.3 = (s32[64]{0:T(128)S(1)}, s32[64]{0:T(128)}, u32[]{:S(2)}) copy-start(s32[64]{0:T(128)} %len_ref.1) | copy-start | bytes 772
  90.8 1.6 copy-start.2
  118.8 3.2 copy-start
